TPU v7x, 1024 devices: a whole 8x8x8 slice. The times are simulated.
1024 devices in a mesh: dp: 8 (over x), mp: 128 (over z, y, core).
Axes of the slice: x: 8, y: 8, z: 8, core: 2. Of those that a mesh axis runs over, the one named last changes fastest.
Arguments:
- rewards: int32 [64], P('dp'), may hold values from 0 to 4096, as said below
- group_ids: int32 [64], P('dp'), may hold values from 0 to 3, as said below
- lengths: int32 [64], P('dp'), may hold values from 1 to 64
- token_mask: int32 [4096], P('dp'), may hold values from 0 to 1, as said below
- targets: int32 [4096], P('dp'), may hold values from 0 to 65535
- logits: bfloat16 [4096, 65536], P('dp', 'mp'), may hold values from -140 to 400
Outputs:
- advantage: float32 [64], P('dp')
- token_weight: float32 [4096], P('dp')
- token_logprob: float32 [4096], P('dp')
- token_entropy: float32 [4096], P('dp')
- objective: float32 [], replicated
Inputs may be any that keep to these rules, and one draw needn't show every extreme that they name: rewards in units of 1/1024. `group_ids`: each of the 4 prompts has exactly 16 trajectories. `token_mask`: zeros come in aligned spans of 8 positions, except that the first position of each window is always 1.
All inputs are finite; a program needn't handle non-finite values.
Results may differ from a plain program's by a relative error of at most 0.00095.
Values may be sent and summed in bfloat16 or wider, within the bound.
No kernel may reach another device: no remote copies, remote signals or barrier semaphores. Data moves between devices by JAX's collectives and lax.ppermute only.
A program may use at most 32 MiB of HBM per device.

v0:
```python
import jax
import jax.numpy as jnp
from jax import lax
from jax.sharding import Mesh
from jax.sharding import PartitionSpec as P

GROUP = 16
WIN = 64
MP = ("mp_0", "mp_1", "mp_2")


spread_floor = 0.25
reward_unit = 1024.0
highest = lax.Precision.HIGHEST


def gathered_once(array, axis):
    leaves = jax.tree.leaves(array)
    sequence = sorted(range(len(leaves)), key=lambda k: -leaves[k].size)
    width = (1, *leaves[sequence[0]].shape)[-1]
    lines = [
        jnp.pad(leaves[k].reshape(-1), (0, -leaves[k].size % width)).reshape(-1, width)
        for k in sequence
    ]
    both, at, found = (lax.all_gather(jnp.concatenate(lines), axis), 0, {})
    for k, line in zip(sequence, lines):
        slab = both[:, at : at + len(line)].reshape(len(both), -1)
        found[k] = slab[:, : leaves[k].size].reshape(-1, *leaves[k].shape)
        at += len(line)
    numbers = iter(range(len(leaves)))
    return jax.tree.map(lambda _: found[next(numbers)], array)


def merged_by_axis(array, axes, combine):
    for axis in axes:
        pieces = gathered_once(array, axis)
        array = jax.tree.map(lambda part: part[0], pieces)
        for k in range(1, lax.axis_size(axis)):
            array = combine(array, jax.tree.map(lambda part: part[k], pieces))
    return array


def over_pieces(array, axis):
    return lax.all_gather(array, axis).sum(0)


def table_dot(left_side, right_side):
    return jnp.dot(left_side, right_side, precision=highest)


def quarter_rows(source, rollouts, quarter, slot_index):
    shaped = source.reshape((rollouts, 4, quarter) + source.shape[1:])
    return shaped[:, slot_index].reshape((rollouts * quarter,) + source.shape[1:])


def join_quarters(pieces, rollouts, quarter):
    stacked = jnp.stack([portion.reshape(rollouts, quarter) for portion in pieces], axis=1)
    return stacked.reshape(rollouts * 4 * quarter)


def tile_peak(logit_tile):
    return jnp.max(logit_tile, axis=1).astype(jnp.float32)


def shifted_sums(logit_tile, row_shift):
    shifted = logit_tile.astype(jnp.float32) - row_shift[:, None]
    weights = jnp.exp(shifted)
    return (jnp.sum(weights, axis=1), jnp.sum(weights * shifted, axis=1))


def own_stats(logit_tile):
    row_peak = tile_peak(logit_tile)
    totals, moments = shifted_sums(logit_tile, row_peak)
    return (row_peak, totals, moments)


def empty_stats(logit_tile):
    height = logit_tile.shape[0]
    return (
        jnp.zeros((height,), jnp.float32),
        jnp.ones((height,), jnp.float32),
        jnp.zeros((height,), jnp.float32),
    )


def merge_stats(left_part, right_part):
    left_peak, left_total, left_moment, left_target = left_part
    right_peak, right_total, right_moment, right_target = right_part
    joint_peak = jnp.maximum(left_peak, right_peak)
    left_factor = jnp.exp(left_peak - joint_peak)
    right_factor = jnp.exp(right_peak - joint_peak)
    joint_total = left_factor * left_total + right_factor * right_total
    joint_moment = left_factor * (
        left_moment + (left_peak - joint_peak) * left_total
    ) + right_factor * (right_moment + (right_peak - joint_peak) * right_total)
    return (joint_peak, joint_total, joint_moment, left_target + right_target)


def shards(rewards, group_ids, lengths, token_mask, targets, logits):
    rollouts = lengths.shape[0]
    vocab_dev = logits.shape[1]
    quarter = WIN // 4
    positions = jnp.arange(WIN, dtype=jnp.int32)
    live_mask = (
        (token_mask.reshape(rollouts, WIN) > 0) & (positions[None, :] < lengths[:, None])
    ).astype(jnp.float32)
    longest = jnp.max(lengths)
    local_index = targets - lax.axis_index(MP) * vocab_dev
    inside = (local_index >= 0) & (local_index < vocab_dev)
    picked = jnp.take_along_axis(logits, jnp.clip(local_index, 0, vocab_dev - 1)[:, None], axis=1)[
        :, 0
    ]
    target_share = jnp.where(inside, picked.astype(jnp.float32), 0.0)
    logit_tiles = [quarter_rows(logits, rollouts, quarter, slot_index) for slot_index in range(4)]
    last_tile = logit_tiles[3]
    last_stats = lax.cond(longest <= 3 * quarter, empty_stats, own_stats, last_tile)
    first_stats = [
        lax.cond(longest > slot_index * quarter, own_stats, empty_stats, logit_tiles[slot_index])
        for slot_index in range(3)
    ]
    every_stats = first_stats + [last_stats]
    joined = tuple(
        (
            join_quarters(
                [stat_group[member_index] for stat_group in every_stats], rollouts, quarter
            )
            for member_index in range(3)
        )
    )
    row_peak, row_total, row_moment, target_logit = merged_by_axis(
        joined + (target_share,), MP, merge_stats
    )
    log_total = row_peak + jnp.log(row_total)
    log_prob = target_logit - log_total
    entropy = jnp.log(row_total) - row_moment / row_total
    token_logprob = live_mask * log_prob.reshape(rollouts, WIN)
    token_entropy = live_mask * entropy.reshape(rollouts, WIN)
    counts = jnp.sum(live_mask, axis=1)
    reward_values = rewards.astype(jnp.float32) / reward_unit
    groups = rollouts * lax.axis_size("dp") // GROUP
    member = (group_ids[:, None] == jnp.arange(groups, dtype=jnp.int32)[None, :]).astype(
        jnp.float32
    )
    rollout_sums = jnp.sum(token_logprob, axis=1)
    sum_reward, sum_square, group_tokens, sum_product, sum_logprob = (
        over_pieces(table_dot(reward_values, member), "dp"),
        over_pieces(table_dot(reward_values * reward_values, member), "dp"),
        over_pieces(table_dot(counts, member), "dp"),
        over_pieces(table_dot(reward_values * rollout_sums, member), "dp"),
        over_pieces(table_dot(rollout_sums, member), "dp"),
    )
    group_mean = sum_reward / GROUP
    group_var = jnp.maximum(sum_square / GROUP - group_mean * group_mean, 0.0)
    group_spread = jnp.maximum(jnp.sqrt(group_var), spread_floor)
    centred = reward_values - table_dot(member, group_mean)
    advantage = centred / table_dot(member, group_spread)
    token_scale = GROUP * WIN / table_dot(member, group_tokens)
    token_weight = live_mask * (advantage * token_scale)[:, None]
    total_rows = groups * GROUP * WIN
    group_terms = (
        GROUP * WIN / group_tokens * (sum_product - group_mean * sum_logprob) / group_spread
    )
    objective = -jnp.sum(group_terms) / total_rows
    return (
        advantage,
        token_weight.reshape(-1),
        token_logprob.reshape(-1),
        token_entropy.reshape(-1),
        objective,
    )


def solution(mesh):
    split = Mesh(mesh.devices.reshape(mesh.shape["dp"], 8, 8, 2), ("dp", "mp_0", "mp_1", "mp_2"))
    in_specs = (P("dp"), P("dp"), P("dp"), P("dp"), P("dp"), P("dp", MP))
    out_specs = (P("dp"), P("dp"), P("dp"), P("dp"), P())
    return jax.shard_map(
        shards, mesh=split, in_specs=in_specs, out_specs=out_specs, check_vma=False
    )
```

profile of v0, /device:TPU:16, one launch (start us, length us, event | category | flops | bytes accessed | tf_op | source)
XLA Modules:
  0.0 117.8 jit_solution(11740585375783513390)
XLA Ops:
  0.6 1.3 %reduce_max.45 = s32[]{:T(128)} reduce(s32[8]{0:T(128)} %param.16, s32[]{:T(128)} %constant.58.clone.1), dimensions={0}, to_apply=%region_4.5 | reduce | flops 7 | bytes 40 | tf_op jit(solution)/shard_map/reduce_max | solution.py:107
  2.6 2.2 %conditional.4 = (f32[8,1,16]{2,0,1:T(8,128)S(1)}, f32[8,1,16]{2,0,1:T(8,128)S(1)}, f32[8,1,16]{2,0,1:T(8,128)S(1)}) conditional(s32[]{:T(128)} %convert_element_type.116, () %tuple.64, bf16[8,4,16,512]{3,2,1,0:T(8,128)(2,1)} %bitcast.697), branch_computations={%region_5.6_spmd, %region_6.0_spmd} | conditional | flops 392960 | bytes 265240 | solution.py:118
  2.6 1.0 slice_reduce_fusion
  3.6 1.1 fusion
  5.4 2.2 %conditional.5 = (f32[8,1,16]{2,0,1:T(8,128)S(1)}, f32[8,1,16]{2,0,1:T(8,128)S(1)}, f32[8,1,16]{2,0,1:T(8,128)S(1)}) conditional(s32[]{:T(128)} %convert_element_type.117, () %tuple.65, bf16[8,4,16,512]{3,2,1,0:T(8,128)(2,1)} %bitcast.698), branch_computations={%region_10.11_spmd, %region_11.15_spmd} | conditional | flops 392960 | bytes 265240 | solution.py:118
  5.4 1.0 slice_reduce_fusion.1
  6.4 1.1 fusion.1
  9.0 0.1 reshape.1964
  9.1 0.1 reshape.1965
  9.2 0.1 reshape.1966
  9.3 0.7 copy-done
  10.0 8.0 %gather_fusion = bf16[512]{0:T(512)(128)(2,1)S(1)} fusion(bf16[512,512]{1,0:T(8,128)(2,1)} %param.19, s32[512]{0:T(512)S(1)} %bitcast.696), kind=kCustom, calls=%fused_computation | custom fusion | bytes 6144 | tf_op jit(solution)/shard_map/jit(take_along_axis)/gather | solution.py:110
  18.1 36.9 %all-gather.8 = f32[8,4,512]{2,1,0:T(4,128)S(1)} all-gather(f32[1,4,512]{2,1,0:T(4,128)S(1)} %maximum_bitcast_fusion), channel_id=5, replica_groups=mesh['dp'=8,'mp_0'=8,'mp_1'=8,'mp_2'=2] {'mp_0'}, dimensions={0}, use_global_device_ids=true | all-gather | bytes 73728 | tf_op jit(solution)/shard_map/all_gather | solution.py:25
  55.0 0.1 fusion.37
  55.2 26.0 %all-gather.9 = f32[8,4,512]{2,1,0:T(4,128)S(1)} all-gather(f32[1,4,512]{2,1,0:T(4,128)S(1)} %maximum_bitcast_fusion.1), channel_id=6, replica_groups=mesh['dp'=8,'mp_0'=8,'mp_1'=8,'mp_2'=2] {'mp_1'}, dimensions={0}, use_global_device_ids=true | all-gather | bytes 73728 | tf_op jit(solution)/shard_map/all_gather | solution.py:25
  81.3 0.1 fusion.13
  81.4 1.8 %all-gather.10 = f32[2,4,512]{2,1,0:T(4,128)S(1)} all-gather(f32[1,4,512]{2,1,0:T(4,128)S(1)} %maximum_bitcast_fusion.2), channel_id=7, replica_groups=mesh['dp'=8,'mp_0'=8,'mp_1'=8,'mp_2'=2] {'mp_2'}, dimensions={0}, use_global_device_ids=true | all-gather | bytes 24576 | tf_op jit(solution)/shard_map/all_gather | solution.py:25
  83.3 0.5 broadcast.197
  83.8 0.7 slice_reduce_fusion.5
  84.5 0.6 copy-done.2
  85.2 0.1 lt.35
  85.3 0.5 copy-done.1
  85.8 0.6 subtract_select_fusion
  86.4 0.1 gt.23
  86.9 0.2 select_reduce_fusion
  87.1 0.7 copy-done.4
  87.7 0.2 convolution_bitcast_fusion
  87.9 1.3 %dynamic-slice = u32[1]{0:T(128)} dynamic-slice(u32[1024]{0:T(1024)} %constant.111, u32[]{:T(128)S(6)} %add.906), dynamic_slice_sizes={1} | dynamic-slice | bytes 12
  89.8 0.2 dynamic-update-slice.4
  90.1 0.4 copy-done.3
  90.5 0.2 convolution_bitcast_fusion.1
  90.7 0.2 dynamic-update-slice.3
  90.9 0.2 convolution_bitcast_fusion.3
  91.1 0.2 dynamic-update-slice.2
  91.2 0.2 convolution_bitcast_fusion.7
  91.4 0.2 dynamic-update-slice
  91.6 0.2 convolution_bitcast_fusion.5
  91.8 0.2 dynamic-update-slice.1
  92.0 21.3 %all-reduce.5 = (f32[32]{0:T(128)S(1)}, f32[32]{0:T(128)S(1)}, f32[32]{0:T(128)S(1)}, f32[32]{0:T(128)S(1)}, f32[32]{0:T(128)S(1)}) all-reduce(f32[32]{0:T(128)S(1)} %dynamic-update-slice.1, f32[32]{0:T(128)S(1)} %dynamic-update-slice, f32[32]{0:T(128)S(1)} %dynamic-update-slice.2, ...), channel_id=3, replica_groups=mesh['dp'=8,'mp_0'=8,'mp_1'=8,'mp_2'=2] {'dp'}, use_global_device_ids=true, to_apply=%add.1 | all-reduce | flops 160 | bytes 1280
  113.3 0.1 reshape.1987
  113.7 0.1 reshape.1994
  113.8 0.6 fusion.107
  115.1 0.2 convolution_bitcast_fusion.4
  115.2 0.2 fusion.5
  115.4 0.2 fusion.7
  115.6 0.3 copy-done.5
  116.0 0.1 mul.1039
  116.1 0.6 subtract_select_fusion.1
  (55 shorter events, 1.3 us)
Async XLA Ops:
  9.3 0.7 copy-start
  84.5 0.7 copy-start.2
  85.1 0.7 copy-start.1
  87.0 0.7 copy-start.4
  89.8 0.7 copy-start.3
  115.4 0.5 copy-start.5
where the time goes:
time: 118 us
  blocking collectives  86 us (73%)
  local copies, waits for them, and re-layouts  15.4 us (13%)
  other arithmetic  8.92 us (8%)
  between operations  5.89 us (5%)
  matrix products  1.49 us (1%)
    all_gather x3, blocking collectives, gathered_once(): both, at, found = (lax.all_gather(jnp.concatenate(lines), axis), 0, {})  64.7 us
    unnamed x1, blocking collectives  21.3 us
    gather x1, local copies, waits for them, and re-layouts, shards(): jnp.take_along_axis(logits, jnp.clip(local_index, 0, vocab_dev - 1)[:, No...  7.99 us
    unnamed x24, local copies, waits for them, and re-layouts  5.55 us

commit v1 on v0

v1 whole, which is shorter than its diff:
```python
import jax
import jax.numpy as jnp
from jax import lax
from jax.experimental import pallas as pl
from jax.experimental.pallas import tpu as pltpu
from jax.sharding import Mesh
from jax.sharding import PartitionSpec as P

GROUP = 16
WIN = 64
LANES = 128
SUBLANES = 8
GROUPS = 4
MP = ("mp_0", "mp_1", "mp_2")

spread_floor = 0.25
reward_unit = 1024.0
highest = lax.Precision.HIGHEST


def lane_of(shape):
    return lax.broadcasted_iota(jnp.int32, shape, 1)


def row_of(shape):
    return lax.broadcasted_iota(jnp.int32, shape, 0)


def placed(contracted, block, precision=None):
    return lax.dot_general(
        contracted,
        block,
        (((1,), (1,)), ((), ())),
        precision=precision,
        preferred_element_type=jnp.float32,
    )


def local_kernel(
    rewards, group_ids, lengths, token_mask, targets, logits,
    send, token_info, own_info,
    tiles, target_rows, mask_rows, reward_of, group_of, length_of, sems,
):
    chunks = logits.shape[0] // LANES
    width = logits.shape[1]
    small = [
        pltpu.make_async_copy(targets, target_rows, sems.at[chunks]),
        pltpu.make_async_copy(token_mask, mask_rows, sems.at[chunks + 1]),
        pltpu.make_async_copy(rewards, reward_of, sems.at[chunks + 2]),
        pltpu.make_async_copy(group_ids, group_of, sems.at[chunks + 3]),
        pltpu.make_async_copy(lengths, length_of, sems.at[chunks + 4]),
    ]
    large = [
        pltpu.make_async_copy(
            logits.at[pl.ds(LANES * c, LANES)], tiles.at[pl.ds(LANES * c, LANES)], sems.at[c]
        )
        for c in range(chunks)
    ]
    small[0].start()
    for copy in large:
        copy.start()
    for copy in small[1:]:
        copy.start()
    column_start = (
        (lax.axis_index("mp_0") * lax.axis_size("mp_1") + lax.axis_index("mp_1"))
        * lax.axis_size("mp_2")
        + lax.axis_index("mp_2")
    ) * width
    for copy in small:
        copy.wait()

    shape = (SUBLANES, LANES)
    row, lane = row_of(shape), lane_of(shape)
    own_row = row == chunks
    reward_info = jnp.zeros(shape, jnp.float32)
    group_info = jnp.zeros(shape, jnp.int32)
    length_info = jnp.zeros(shape, jnp.int32)
    for i in range(2 * chunks):
        here = ((row == i // 2) & (lane // WIN == i % 2)) | (own_row & (lane == i))
        reward_info = jnp.where(here, reward_of[i].astype(jnp.float32), reward_info)
        group_info = jnp.where(here, group_of[i], group_info)
        length_info = jnp.where(here, length_of[i], length_info)
    reward_info = reward_info / reward_unit
    mask8 = jnp.concatenate([mask_rows[...], mask_rows[...]], axis=0)
    live = jnp.where((row < chunks) & (mask8 > 0) & (lane % WIN < length_info), 1.0, 0.0)
    token_info[0] = live
    token_info[1] = reward_info
    token_info[2] = group_info.astype(jnp.float32)
    even = jnp.sum(jnp.where(lane < WIN, live, 0.0), axis=1, keepdims=True)
    odd = jnp.sum(jnp.where(lane >= WIN, live, 0.0), axis=1, keepdims=True)
    spread_out = jnp.where((row == lane // 2) & (row < chunks), jnp.where(lane % 2 == 0, even, odd), 0.0)
    counts = jnp.sum(spread_out, axis=0, keepdims=True)
    own_reward = jnp.where(lane < 2 * chunks, reward_info[chunks : chunks + 1], 0.0)
    own_group = jnp.where(lane < 2 * chunks, group_info[chunks : chunks + 1].astype(jnp.float32), 0.0)
    own_info[...] = jnp.where(
        row == 1, counts, jnp.where(row == 2, own_reward, jnp.where(row == 3, own_group, 0.0))
    )

    block = (LANES, LANES)
    block_lane = lane_of(block)
    exact_tile = jnp.zeros(shape, jnp.float32)
    sum_tile = jnp.zeros(shape, jnp.float32)
    two_row, two_lane = row_of((SUBLANES, 2 * LANES)), lane_of((SUBLANES, 2 * LANES))
    for c in range(chunks):
        target_block = jnp.broadcast_to(target_rows[c : c + 1, :] - column_start, block).T
        large[c].wait()
        logit_block = tiles[LANES * c : LANES * (c + 1), :].astype(jnp.float32)
        row_peak = jnp.max(logit_block, axis=1, keepdims=True)
        totals = jnp.zeros(block, jnp.float32)
        moments = jnp.zeros(block, jnp.float32)
        picked = jnp.zeros(block, jnp.float32)
        for k in range(width // LANES):
            part = logit_block[:, LANES * k : LANES * (k + 1)]
            shifted = part - row_peak
            weights = jnp.exp(shifted)
            totals += weights
            moments += weights * shifted
            picked += jnp.where(target_block == block_lane + LANES * k, part, 0.0)
        peaks = jnp.broadcast_to(row_peak, block)
        exact_pick = jnp.where(
            ((two_row == c) & (two_lane == 0)) | ((two_row == chunks + c) & (two_lane >= LANES)), 1.0, 0.0
        )
        sum_pick = jnp.where(
            ((two_row == c) & (two_lane < LANES)) | ((two_row == chunks + c) & (two_lane >= LANES)), 1.0, 0.0
        )
        exact_tile += placed(
            exact_pick.astype(jnp.bfloat16),
            jnp.concatenate([peaks, picked], axis=1).astype(jnp.bfloat16),
        )
        sum_tile += placed(sum_pick, jnp.concatenate([totals, moments], axis=1), highest)
    for n in range(send.shape[0]):
        send[n, :SUBLANES] = exact_tile
        send[n, SUBLANES:] = sum_tile


def merged(received):
    shape = (SUBLANES, LANES)
    half = SUBLANES // 2
    upper = row_of(shape) < half
    heads = [received[n, :SUBLANES] for n in range(received.shape[0])]
    peaks = [jnp.where(upper, head, pltpu.roll(head, half, 0)) for head in heads]
    picked = sum(heads[1:], heads[0])
    joint = peaks[0]
    for peak in peaks[1:]:
        joint = jnp.maximum(joint, peak)
    sums = jnp.zeros(shape, jnp.float32)
    extra = jnp.zeros(shape, jnp.float32)
    for n, peak in enumerate(peaks):
        shift = peak - joint
        scaled = jnp.exp(shift) * received[n, SUBLANES:]
        sums += scaled
        extra += shift * scaled
    sums += jnp.where(upper, 0.0, pltpu.roll(extra, half, 0))
    return joint, picked, sums


def merge_kernel(received, send):
    joint, picked, sums = merged(received)
    upper = row_of((SUBLANES, LANES)) < SUBLANES // 2
    head = jnp.where(upper, joint, picked)
    for n in range(send.shape[0]):
        send[n, :SUBLANES] = head
        send[n, SUBLANES:] = sums


def token_kernel(received, token_info, own_info, send, token_values):
    half = SUBLANES // 2
    shape = (SUBLANES, LANES)
    row, lane = row_of(shape), lane_of(shape)
    upper = row < half
    joint, picked, sums = merged(received)
    target = pltpu.roll(picked, half, 0)
    moment = pltpu.roll(sums, half, 0)
    total = jnp.where(upper, sums, 1.0)
    log_sum = jnp.log(total)
    live = token_info[0]
    logprob = live * (target - (joint + log_sum))
    entropy = live * (log_sum - moment / total)
    token_values[:half] = logprob[:half]
    token_values[half:] = entropy[:half]
    logprob = jnp.where(upper, logprob, 0.0)
    even = jnp.sum(jnp.where(lane < WIN, logprob, 0.0), axis=1, keepdims=True)
    odd = jnp.sum(jnp.where(lane >= WIN, logprob, 0.0), axis=1, keepdims=True)
    spread_out = jnp.where((row == lane // 2) & upper, jnp.where(lane % 2 == 0, even, odd), 0.0)
    packed = jnp.where(row == 0, jnp.sum(spread_out, axis=0, keepdims=True), own_info[...])
    for n in range(send.shape[0]):
        send[n] = packed


def final_kernel(
    received, token_info, token_values,
    advantage, token_weight, token_logprob, token_entropy, objective,
    advantage_row, weight_rows, objective_row, sems,
):
    half = SUBLANES // 2
    copies = [
        pltpu.make_async_copy(token_values.at[pl.ds(0, half)], token_logprob, sems.at[0]),
        pltpu.make_async_copy(token_values.at[pl.ds(half, half)], token_entropy, sems.at[1]),
        pltpu.make_async_copy(weight_rows, token_weight, sems.at[2]),
        pltpu.make_async_copy(advantage_row, advantage, sems.at[3]),
        pltpu.make_async_copy(objective_row, objective, sems.at[4]),
    ]
    copies[0].start()
    copies[1].start()
    shape = (SUBLANES, LANES)
    row, lane = row_of(shape), lane_of(shape)
    own = received.shape[0]
    gathered = received[0]
    for d in range(1, own):
        gathered += pltpu.roll(received[d], SUBLANES * d, 1)
    logprob_sums, counts = gathered[0:1], gathered[1:2]
    reward_values, groups = gathered[2:3], gathered[3:4]
    slot = row % GROUPS
    first = row < GROUPS
    member = (groups == slot.astype(jnp.float32)) & (lane < SUBLANES * own)
    sums = jnp.sum(
        jnp.where(member, jnp.where(first, reward_values, counts), 0.0), axis=1, keepdims=True
    )
    group_mean = sums / GROUP

    def spread_over(chosen, values):
        return jnp.sum(jnp.where(member & chosen, values, 0.0), axis=0, keepdims=True)

    centred = reward_values - spread_over(first, group_mean)
    group_var = (
        jnp.sum(jnp.where(member & first, centred * centred, 0.0), axis=1, keepdims=True) / GROUP
    )
    group_spread = jnp.maximum(jnp.sqrt(group_var), spread_floor)
    live_rollouts = lane[0:1] < SUBLANES * own
    spread_row = jnp.where(live_rollouts, spread_over(first, group_spread), 1.0)
    tokens_row = jnp.where(live_rollouts, spread_over(~first, sums), 1.0)
    weights = centred / spread_row * (GROUP * WIN / tokens_row)
    products = jnp.where(live_rollouts, weights * logprob_sums, 0.0)
    total_rows = GROUPS * GROUP * WIN
    objective_row[...] = -jnp.sum(products, axis=1, keepdims=True) / total_rows
    copies[4].start()

    info_reward, info_group = token_info[1], token_info[2]
    mean, spread, tokens = group_mean[0:1], group_spread[0:1], sums[GROUPS : GROUPS + 1]
    for g in range(1, GROUPS):
        here = info_group == float(g)
        mean = jnp.where(here, group_mean[g : g + 1], mean)
        spread = jnp.where(here, group_spread[g : g + 1], spread)
        tokens = jnp.where(here, sums[GROUPS + g : GROUPS + g + 1], tokens)
    info_advantage = (info_reward - mean) / spread
    weight = token_info[0] * (info_advantage * (GROUP * WIN / tokens))
    advantage_row[...] = info_advantage[half : half + 1, :SUBLANES]
    copies[3].start()
    weight_rows[...] = weight[:half]
    copies[2].start()
    for copy in copies:
        copy.wait()


def shards(rewards, group_ids, lengths, token_mask, targets, logits):
    rows = logits.shape[0]
    chunks = rows // LANES
    f32, i32 = jnp.float32, jnp.int32
    any_spec = pl.BlockSpec(memory_space=pl.ANY)
    vmem = pl.BlockSpec(memory_space=pltpu.VMEM)
    stat_shape = (2 * SUBLANES, LANES)
    first_axes = ("mp_0", "mp_2")
    first_size = lax.axis_size("mp_0") * lax.axis_size("mp_2")
    sent, token_info, own_info = pl.pallas_call(
        local_kernel,
        name="local_stats",
        in_specs=[any_spec] * 6,
        out_specs=[vmem] * 3,
        out_shape=[
            jax.ShapeDtypeStruct((first_size, *stat_shape), f32),
            jax.ShapeDtypeStruct((3, SUBLANES, LANES), f32),
            jax.ShapeDtypeStruct((SUBLANES, LANES), f32),
        ],
        scratch_shapes=[
            pltpu.VMEM(logits.shape, logits.dtype),
            pltpu.VMEM((chunks, LANES), i32),
            pltpu.VMEM((chunks, LANES), i32),
            pltpu.SMEM(rewards.shape, i32),
            pltpu.SMEM(rewards.shape, i32),
            pltpu.SMEM(rewards.shape, i32),
            pltpu.SemaphoreType.DMA((chunks + 5,)),
        ],
    )(
        rewards,
        group_ids,
        lengths,
        token_mask.reshape(chunks, LANES),
        targets.reshape(chunks, LANES),
        logits,
    )
    received = lax.all_to_all(sent, first_axes, 0, 0, tiled=True)
    sent = pl.pallas_call(
        merge_kernel,
        name="merge_stats",
        in_specs=[vmem],
        out_specs=vmem,
        out_shape=jax.ShapeDtypeStruct((lax.axis_size("mp_1"), *stat_shape), f32),
    )(received)
    received = lax.all_to_all(sent, "mp_1", 0, 0, tiled=True)
    sent, token_values = pl.pallas_call(
        token_kernel,
        name="token_values",
        in_specs=[vmem] * 3,
        out_specs=[vmem] * 2,
        out_shape=[
            jax.ShapeDtypeStruct((lax.axis_size("dp"), SUBLANES, LANES), f32),
            jax.ShapeDtypeStruct((2 * chunks, LANES), f32),
        ],
    )(received, token_info, own_info)
    received = lax.all_to_all(sent, "dp", 0, 0, tiled=True)
    advantage, token_weight, token_logprob, token_entropy, objective = pl.pallas_call(
        final_kernel,
        name="group_values",
        in_specs=[vmem] * 3,
        out_specs=[any_spec] * 5,
        out_shape=[
            jax.ShapeDtypeStruct((1, SUBLANES), f32),
            jax.ShapeDtypeStruct((chunks, LANES), f32),
            jax.ShapeDtypeStruct((chunks, LANES), f32),
            jax.ShapeDtypeStruct((chunks, LANES), f32),
            jax.ShapeDtypeStruct((1, 1), f32),
        ],
        scratch_shapes=[
            pltpu.VMEM((1, SUBLANES), f32),
            pltpu.VMEM((chunks, LANES), f32),
            pltpu.VMEM((1, 1), f32),
            pltpu.SemaphoreType.DMA((5,)),
        ],
    )(received, token_info, token_values)
    return (
        advantage.reshape(-1),
        token_weight.reshape(-1),
        token_logprob.reshape(-1),
        token_entropy.reshape(-1),
        objective.reshape(()),
    )


def solution(mesh):
    split = Mesh(mesh.devices.reshape(mesh.shape["dp"], 8, 8, 2), ("dp", "mp_0", "mp_1", "mp_2"))
    in_specs = (P("dp"), P("dp"), P("dp"), P("dp"), P("dp"), P("dp", MP))
    out_specs = (P("dp"), P("dp"), P("dp"), P("dp"), P())
    return jax.shard_map(
        shards, mesh=split, in_specs=in_specs, out_specs=out_specs, check_vma=False
    )
```

time: 118 us -> 65.1 us (0.55)
  the two profiles are of different devices: /device:TPU:16 before, /device:TPU:1 now
where the time goes in v1:
time: 65.1 us; the launch traced here: 64.2 us
  blocking collectives  55.2 us (85%)
  Pallas kernels  8.34 us (13%)
    all_to_all x1, blocking collectives, shards(): received = lax.all_to_all(sent, first_axes, 0, 0, tiled=True)  27.2 us
    all_to_all x1, blocking collectives, shards(): received = lax.all_to_all(sent, 'mp_1', 0, 0, tiled=True)  14.5 us
    all_to_all x1, blocking collectives, shards(): received = lax.all_to_all(sent, 'dp', 0, 0, tiled=True)  13.5 us
    pallas_call x1, Pallas kernels, shards(): pl.pallas_call(local_kernel, name='local_stats', in_specs=[any_spec] * 6,...  3.4 us
    pallas_call x1, Pallas kernels, shards(): pl.pallas_call(final_kernel, name='group_values', in_specs=[vmem] * 3, ou...  1.75 us
    pallas_call x1, Pallas kernels, shards(): pl.pallas_call(token_kernel, name='token_values', in_specs=[vmem] * 3, ou...  1.6 us
    pallas_call x1, Pallas kernels, shards(): pl.pallas_call(merge_kernel, name='merge_stats', in_specs=[vmem], out_spe...  1.58 us

profile of v1, /device:TPU:1, one launch (start us, length us, event | category | flops | bytes accessed | tf_op | source)
XLA Modules:
  0.0 64.2 jit_solution(14211208634482486036)
XLA Ops:
  0.6 3.4 %local_stats.1 = (f32[16,16,128]{2,1,0:T(8,128)}, f32[3,8,128]{2,1,0:T(8,128)}, f32[8,128]{1,0:T(8,128)}) custom-call(s32[8]{0:T(128)} %rewards.1, s32[8]{0:T(128)} %group_ids.1, s32[8]{0:T(128)} %lengths.1, s32[4,128]{1,0:T(4,128)} %bitcast.7, s32[4,128]{1,0:T(4,128)} %bitcast.8, bf16[512,512]{1,0:T(8,128)(2,1)} %logits.1), custom_call_target="tpu_custom_call" | custom-call | tf_op jit(solution)/shard_map/local_stats/pallas_call | solution.py:264
  4.0 27.2 %all_to_all.15.received = f32[16,16,128]{2,1,0:T(8,128)} all-to-all(f32[16,16,128]{2,1,0:T(8,128)} %get-tuple-element.15), channel_id=1, replica_groups=mesh['dp'=8,'mp_0'=8,'mp_1'=8,'mp_2'=2] {'mp_0','mp_2'}, dimensions={0} | all-to-all | bytes 262144 | tf_op jit(solution)/shard_map/all_to_all | solution.py:291
  31.2 1.6 %merge_stats.1 = f32[8,16,128]{2,1,0:T(8,128)} custom-call(f32[16,16,128]{2,1,0:T(8,128)} %all_to_all.15.received), custom_call_target="tpu_custom_call" | custom-call | tf_op jit(solution)/shard_map/merge_stats/pallas_call | solution.py:292
  32.8 14.5 %all_to_all.16.received = f32[8,16,128]{2,1,0:T(8,128)} all-to-all(f32[8,16,128]{2,1,0:T(8,128)} %merge_stats.1), channel_id=1, replica_groups=mesh['dp'=8,'mp_0'=8,'mp_1'=8,'mp_2'=2] {'mp_1'}, dimensions={0} | all-to-all | bytes 131072 | tf_op jit(solution)/shard_map/all_to_all | solution.py:299
  47.3 1.6 %token_values.1 = (f32[8,8,128]{2,1,0:T(8,128)}, f32[8,128]{1,0:T(8,128)}) custom-call(f32[8,16,128]{2,1,0:T(8,128)} %all_to_all.16.received, f32[3,8,128]{2,1,0:T(8,128)} %get-tuple-element.16.token_info, f32[8,128]{1,0:T(8,128)} %get-tuple-element.17.own_info), custom_call_target="tpu_custom_call" | custom-call | tf_op jit(solution)/shard_map/token_values/pallas_call | solution.py:300
  48.9 13.5 %all_to_all.17.received = f32[8,8,128]{2,1,0:T(8,128)} all-to-all(f32[8,8,128]{2,1,0:T(8,128)} %get-tuple-element.18), channel_id=1, replica_groups=mesh['dp'=8,'mp_0'=8,'mp_1'=8,'mp_2'=2] {'dp'}, dimensions={0} | all-to-all | bytes 65536 | tf_op jit(solution)/shard_map/all_to_all | solution.py:310
  62.4 1.8 %group_values.1 = (f32[1,8]{1,0:T(1,128)}, f32[4,128]{1,0:T(4,128)}, f32[4,128]{1,0:T(4,128)}, f32[4,128]{1,0:T(4,128)}, f32[1,1]{1,0:T(1,128)}) custom-call(f32[8,8,128]{2,1,0:T(8,128)} %all_to_all.17.received, f32[3,8,128]{2,1,0:T(8,128)} %get-tuple-element.16.token_info, f32[8,128]{1,0:T(8,128)} %get-tuple-element.19.token_values), custom_call_target="tpu_custom_call" | custom-call | tf_op jit(solution)/shard_map/group_values/pallas_call | solution.py:311

commit v2 on v1

--- a/solution.py
+++ b/solution.py
@@ -257,6 +257,13 @@
     chunks = rows // LANES
     f32, i32 = jnp.float32, jnp.int32
     any_spec = pl.BlockSpec(memory_space=pl.ANY)
+
+    def kept(shape):
+        return pltpu.VMEM(shape, f32)
+
+    def near(array):
+        return pltpu.with_memory_space_constraint(array, pltpu.VMEM)
+
     vmem = pl.BlockSpec(memory_space=pltpu.VMEM)
     stat_shape = (2 * SUBLANES, LANES)
     first_axes = ("mp_0", "mp_2")
@@ -267,9 +274,9 @@
         in_specs=[any_spec] * 6,
         out_specs=[vmem] * 3,
         out_shape=[
-            jax.ShapeDtypeStruct((first_size, *stat_shape), f32),
-            jax.ShapeDtypeStruct((3, SUBLANES, LANES), f32),
-            jax.ShapeDtypeStruct((SUBLANES, LANES), f32),
+            kept((first_size, *stat_shape)),
+            kept((3, SUBLANES, LANES)),
+            kept((SUBLANES, LANES)),
         ],
         scratch_shapes=[
             pltpu.VMEM(logits.shape, logits.dtype),
@@ -294,8 +301,8 @@
         name="merge_stats",
         in_specs=[vmem],
         out_specs=vmem,
-        out_shape=jax.ShapeDtypeStruct((lax.axis_size("mp_1"), *stat_shape), f32),
-    )(received)
+        out_shape=kept((lax.axis_size("mp_1"), *stat_shape)),
+    )(near(received))
     received = lax.all_to_all(sent, "mp_1", 0, 0, tiled=True)
     sent, token_values = pl.pallas_call(
         token_kernel,
@@ -303,10 +310,10 @@
         in_specs=[vmem] * 3,
         out_specs=[vmem] * 2,
         out_shape=[
-            jax.ShapeDtypeStruct((lax.axis_size("dp"), SUBLANES, LANES), f32),
-            jax.ShapeDtypeStruct((2 * chunks, LANES), f32),
-        ],
-    )(received, token_info, own_info)
+            kept((lax.axis_size("dp"), SUBLANES, LANES)),
+            kept((2 * chunks, LANES)),
+        ],
+    )(near(received), near(token_info), near(own_info))
     received = lax.all_to_all(sent, "dp", 0, 0, tiled=True)
     advantage, token_weight, token_logprob, token_entropy, objective = pl.pallas_call(
         final_kernel,
@@ -326,7 +333,7 @@
             pltpu.VMEM((1, 1), f32),
             pltpu.SemaphoreType.DMA((5,)),
         ],
-    )(received, token_info, token_values)
+    )(near(received), near(token_info), near(token_values))
     return (
         advantage.reshape(-1),
         token_weight.reshape(-1),

time: 65.1 us -> 59.5 us (0.914)
  Pallas kernels: 8.34 us -> 3.9 us
  blocking collectives: 55.2 us -> 54.2 us
    pallas_call x1, Pallas kernels: 1.58 us -> 0.05 us  [shards(): pl.pallas_call(merge_kernel, name='merge_stats', in_specs=[vmem], out_spe...]
    pallas_call x1, Pallas kernels: 1.6 us -> 0.12 us  [shards(): pl.pallas_call(token_kernel, name='token_values', in_specs=[vmem] * 3, ou...]
    pallas_call x1, Pallas kernels: 1.75 us -> 0.98 us  [shards(): pl.pallas_call(final_kernel, name='group_values', in_specs=[vmem] * 3, ou...]
where the time goes in v2:
time: 59.5 us; the launch traced here: 58.8 us
  blocking collectives  54.2 us (91%)
  Pallas kernels  3.9 us (7%)
  between operations  0.64 us (1%)
    all_to_all x1, blocking collectives, shards(): received = lax.all_to_all(sent, first_axes, 0, 0, tiled=True)  26.9 us
    all_to_all x1, blocking collectives, shards(): received = lax.all_to_all(sent, 'mp_1', 0, 0, tiled=True)  14.2 us
    all_to_all x1, blocking collectives, shards(): received = lax.all_to_all(sent, 'dp', 0, 0, tiled=True)  13.2 us
    pallas_call x1, Pallas kernels, shards(): pl.pallas_call(local_kernel, name='local_stats', in_specs=[any_spec] * 6,...  2.76 us

profile of v2, /device:TPU:1, one launch (start us, length us, event | category | flops | bytes accessed | tf_op | source)
XLA Modules:
  0.0 58.8 jit_solution(9555125722559077869)
XLA Ops:
  0.6 2.8 %local_stats.1 = (f32[16,16,128]{2,1,0:T(8,128)S(1)}, f32[3,8,128]{2,1,0:T(8,128)S(1)}, f32[8,128]{1,0:T(8,128)S(1)}) custom-call(s32[8]{0:T(128)} %rewards.1, s32[8]{0:T(128)} %group_ids.1, s32[8]{0:T(128)} %lengths.1, s32[4,128]{1,0:T(4,128)} %bitcast.7, s32[4,128]{1,0:T(4,128)} %bitcast.8, bf16[512,512]{1,0:T(8,128)(2,1)} %logits.1), custom_call_target="tpu_custom_call" | custom-call | tf_op jit(solution)/shard_map/local_stats/pallas_call | solution.py:271
  3.4 26.9 %all_to_all.15.received = f32[16,16,128]{2,1,0:T(8,128)S(1)} all-to-all(f32[16,16,128]{2,1,0:T(8,128)S(1)} %get-tuple-element.15), channel_id=1, replica_groups=mesh['dp'=8,'mp_0'=8,'mp_1'=8,'mp_2'=2] {'mp_0','mp_2'}, dimensions={0} | all-to-all | bytes 262144 | tf_op jit(solution)/shard_map/all_to_all | solution.py:298
  30.3 0.1 merge_stats.1
  30.3 14.2 %all_to_all.16.received = f32[8,16,128]{2,1,0:T(8,128)S(1)} all-to-all(f32[8,16,128]{2,1,0:T(8,128)S(1)} %merge_stats.1), channel_id=1, replica_groups=mesh['dp'=8,'mp_0'=8,'mp_1'=8,'mp_2'=2] {'mp_1'}, dimensions={0} | all-to-all | bytes 131072 | tf_op jit(solution)/shard_map/all_to_all | solution.py:306
  44.5 0.1 token_values.1
  44.7 13.2 %all_to_all.17.received = f32[8,8,128]{2,1,0:T(8,128)S(1)} all-to-all(f32[8,8,128]{2,1,0:T(8,128)S(1)} %get-tuple-element.18), channel_id=1, replica_groups=mesh['dp'=8,'mp_0'=8,'mp_1'=8,'mp_2'=2] {'dp'}, dimensions={0} | all-to-all | bytes 65536 | tf_op jit(solution)/shard_map/all_to_all | solution.py:317
  57.8 1.0 %group_values.1 = (f32[1,8]{1,0:T(1,128)}, f32[4,128]{1,0:T(4,128)}, f32[4,128]{1,0:T(4,128)}, f32[4,128]{1,0:T(4,128)}, f32[1,1]{1,0:T(1,128)}) custom-call(f32[8,8,128]{2,1,0:T(8,128)S(1)} %all_to_all.17.received, f32[3,8,128]{2,1,0:T(8,128)S(1)} %get-tuple-element.16.token_info, f32[8,128]{1,0:T(8,128)S(1)} %get-tuple-element.19.token_values), custom_call_target="tpu_custom_call" | custom-call | tf_op jit(solution)/shard_map/group_values/pallas_call | solution.py:318

commit v3 on v2

v3 whole, which is shorter than its diff:
```python
import jax
import jax.numpy as jnp
from jax import lax
from jax.experimental import pallas as pl
from jax.experimental.pallas import tpu as pltpu
from jax.sharding import Mesh
from jax.sharding import PartitionSpec as P

GROUP = 16
WIN = 64
LANES = 128
SUBLANES = 8
GROUPS = 4
MP = ("mp_0", "mp_1", "mp_2")

spread_floor = 0.25
reward_unit = 1024.0
highest = lax.Precision.HIGHEST


def lane_of(shape):
    return lax.broadcasted_iota(jnp.int32, shape, 1)


def row_of(shape):
    return lax.broadcasted_iota(jnp.int32, shape, 0)


def placed(contracted, block, precision=None):
    return lax.dot_general(
        contracted,
        block,
        (((1,), (1,)), ((), ())),
        precision=precision,
        preferred_element_type=jnp.float32,
    )


def local_kernel(
    rewards, group_ids, lengths, token_mask, targets, logits,
    send, token_info, own_info,
    tiles, target_rows, mask_rows, reward_of, group_of, length_of, sems,
):
    chunks = logits.shape[0] // LANES
    width = logits.shape[1]
    cores = lax.axis_size("mp_2")
    core = lax.axis_index("mp_2")
    part = chunks // cores
    small = [
        pltpu.make_async_copy(targets, target_rows, sems.at[chunks]),
        pltpu.make_async_copy(token_mask, mask_rows, sems.at[chunks + 1]),
        pltpu.make_async_copy(rewards, reward_of, sems.at[chunks + 2]),
        pltpu.make_async_copy(group_ids, group_of, sems.at[chunks + 3]),
        pltpu.make_async_copy(lengths, length_of, sems.at[chunks + 4]),
    ]
    large = [
        pltpu.make_async_copy(
            logits.at[pl.ds(LANES * c, LANES)], tiles.at[pl.ds(LANES * c, LANES)], sems.at[c]
        )
        for c in range(chunks)
    ]
    small[0].start()
    for copy in large:
        copy.start()
    for copy in small[1:]:
        copy.start()
    column_start = (
        (lax.axis_index("mp_0") * lax.axis_size("mp_1") + lax.axis_index("mp_1")) * cores + core
    ) * width
    small[0].wait()

    shape = (SUBLANES, LANES)
    block = (LANES, LANES)
    block_lane = lane_of(block)
    exact_row, exact_lane = row_of((SUBLANES, 2 * LANES)), lane_of((SUBLANES, 2 * LANES))
    packed = []
    for c in range(chunks):
        k_row = c % part
        target_block = jnp.broadcast_to(target_rows[c : c + 1, :] - column_start, block).T
        large[c].wait()
        logit_block = tiles[LANES * c : LANES * (c + 1), :].astype(jnp.float32)
        row_peak = jnp.max(logit_block, axis=1, keepdims=True)
        totals = jnp.zeros(block, jnp.float32)
        moments = jnp.zeros(block, jnp.float32)
        picked = jnp.zeros(block, jnp.float32)
        for k in range(width // LANES):
            segment = logit_block[:, LANES * k : LANES * (k + 1)]
            shifted = segment - row_peak
            weights = jnp.exp(shifted)
            totals += weights
            moments += weights * shifted
            picked += jnp.where(target_block == block_lane + LANES * k, segment, 0.0)
        peaks = jnp.broadcast_to(row_peak, block)
        exact_pick = jnp.where(
            ((exact_row == k_row) & (exact_lane == 0))
            | ((exact_row == part + k_row) & (exact_lane >= LANES)),
            1.0,
            0.0,
        )
        sum_pick = jnp.where(
            ((exact_row == 2 * part + k_row) & (exact_lane < LANES))
            | ((exact_row == 3 * part + k_row) & (exact_lane >= LANES)),
            1.0,
            0.0,
        )
        tile = placed(
            exact_pick.astype(jnp.bfloat16),
            jnp.concatenate([peaks, picked], axis=1).astype(jnp.bfloat16),
        ) + placed(sum_pick, jnp.concatenate([totals, moments], axis=1), highest)
        if k_row == 0:
            packed.append(tile)
        else:
            packed[-1] += tile
    for n in range(send.shape[0]):
        send[n] = packed[n % cores]

    for copy in small[1:]:
        copy.wait()
    row, lane = row_of(shape), lane_of(shape)
    own_row = row == chunks
    reward_info = jnp.zeros(shape, jnp.float32)
    group_info = jnp.zeros(shape, jnp.int32)
    length_info = jnp.zeros(shape, jnp.int32)
    for i in range(2 * chunks):
        here = ((row == i // 2) & (lane // WIN == i % 2)) | (own_row & (lane == i))
        reward_info = jnp.where(here, reward_of[i].astype(jnp.float32), reward_info)
        group_info = jnp.where(here, group_of[i], group_info)
        length_info = jnp.where(here, length_of[i], length_info)
    reward_info = reward_info / reward_unit
    mask8 = jnp.concatenate([mask_rows[...], mask_rows[...]], axis=0)
    live = jnp.where((row < chunks) & (mask8 > 0) & (lane % WIN < length_info), 1.0, 0.0)
    token_info[0] = live
    token_info[1] = reward_info
    token_info[2] = group_info.astype(jnp.float32)
    token_info[3] = jnp.where(core == 0, live, pltpu.roll(live, SUBLANES - part, 0))
    even = jnp.sum(jnp.where(lane < WIN, live, 0.0), axis=1, keepdims=True)
    odd = jnp.sum(jnp.where(lane >= WIN, live, 0.0), axis=1, keepdims=True)
    spread_out = jnp.where(
        (row == lane // 2) & (row < chunks), jnp.where(lane % 2 == 0, even, odd), 0.0
    )
    counts = jnp.sum(spread_out, axis=0, keepdims=True)
    own_reward = jnp.where(lane < 2 * chunks, reward_info[chunks : chunks + 1], 0.0)
    own_group = jnp.where(
        lane < 2 * chunks, group_info[chunks : chunks + 1].astype(jnp.float32), 0.0
    )
    own_info[...] = jnp.where(
        row == 5, counts, jnp.where(row == 6, own_reward, jnp.where(row == 7, own_group, 0.0))
    )


def merged(received):
    shape = (SUBLANES, LANES)
    row = row_of(shape)
    tiles = [received[n] for n in range(received.shape[0])]
    peaks = [
        jnp.where(
            row < 2,
            tile,
            jnp.where(
                row < 4,
                pltpu.roll(tile, 2, 0),
                jnp.where(row < 6, pltpu.roll(tile, 4, 0), pltpu.roll(tile, 6, 0)),
            ),
        )
        for tile in tiles
    ]
    joint = peaks[0]
    for peak in peaks[1:]:
        joint = jnp.maximum(joint, peak)
    sums = jnp.zeros(shape, jnp.float32)
    extra = jnp.zeros(shape, jnp.float32)
    for tile, peak in zip(tiles, peaks):
        shift = peak - joint
        scaled = jnp.exp(shift) * tile
        sums += jnp.where(row < 4, tile, scaled)
        extra += shift * scaled
    sums += jnp.where(row < 6, 0.0, pltpu.roll(extra, 2, 0))
    return jnp.where(row < 2, joint, sums)


def merge_kernel(received, send):
    tile = merged(received)
    for n in range(send.shape[0]):
        send[n] = tile


def token_kernel(received, token_info, own_info, send):
    shape = (SUBLANES, LANES)
    row, lane = row_of(shape), lane_of(shape)
    part = token_info.shape[1] // 2 // lax.axis_size("mp_2")
    first = 2 * part * lax.axis_index("mp_2")
    tile = merged(received)
    upper = row < part
    target = pltpu.roll(tile, 6, 0)
    total = jnp.where(upper, pltpu.roll(tile, 4, 0), 1.0)
    moment = pltpu.roll(tile, 2, 0)
    log_sum = jnp.log(total)
    live = token_info[3]
    logprob = jnp.where(upper, live * (target - (tile + log_sum)), 0.0)
    entropy = jnp.where(upper, live * (log_sum - moment / total), 0.0)
    even = jnp.sum(jnp.where(lane < WIN, logprob, 0.0), axis=1, keepdims=True)
    odd = jnp.sum(jnp.where(lane >= WIN, logprob, 0.0), axis=1, keepdims=True)
    own_lane = lane - first
    spread_out = jnp.where(
        (own_lane >= 0) & (row == own_lane // 2) & upper,
        jnp.where(lane % 2 == 0, even, odd),
        0.0,
    )
    packed = jnp.where(
        upper,
        logprob,
        jnp.where(
            row < 4,
            pltpu.roll(entropy, 2, 0),
            jnp.where(row == 4, jnp.sum(spread_out, axis=0, keepdims=True), own_info[...]),
        ),
    )
    for n in range(send.shape[0]):
        send[n] = packed


def final_kernel(
    received, token_info,
    advantage, token_weight, token_logprob, token_entropy, objective,
    advantage_row, weight_rows, logprob_rows, entropy_rows, objective_row, sems,
):
    chunks = token_weight.shape[0]
    copies = [
        pltpu.make_async_copy(logprob_rows, token_logprob, sems.at[0]),
        pltpu.make_async_copy(entropy_rows, token_entropy, sems.at[1]),
        pltpu.make_async_copy(weight_rows, token_weight, sems.at[2]),
        pltpu.make_async_copy(advantage_row, advantage, sems.at[3]),
        pltpu.make_async_copy(objective_row, objective, sems.at[4]),
    ]
    shape = (SUBLANES, LANES)
    row, lane = row_of(shape), lane_of(shape)
    shards = lax.axis_size("dp")
    here = 2 * lax.axis_index("dp")
    low, high = received[here], received[here + 1]
    logprob_rows[...] = jnp.where(row < 2, low, pltpu.roll(high, 2, 0))[:chunks]
    copies[0].start()
    entropy_rows[...] = jnp.where(row < 2, pltpu.roll(low, 6, 0), high)[:chunks]
    copies[1].start()
    gathered = jnp.zeros(shape, jnp.float32)
    for d in range(shards):
        pair = received[2 * d] + jnp.where(row == 4, received[2 * d + 1], 0.0)
        gathered += pltpu.roll(pair, SUBLANES * d, 1) if d else pair
    valid = lane < SUBLANES * shards
    logprob_sums, counts = gathered[4:5], gathered[5:6]
    reward_values, groups = gathered[6:7], gathered[7:8]
    slot = row % GROUPS
    first = row < GROUPS
    member = (groups == slot.astype(jnp.float32)) & valid
    sums = jnp.sum(
        jnp.where(member, jnp.where(first, reward_values, counts), 0.0), axis=1, keepdims=True
    )
    group_mean = sums / GROUP

    def spread_over(chosen, values):
        return jnp.sum(jnp.where(member & chosen, values, 0.0), axis=0, keepdims=True)

    centred = reward_values - spread_over(first, group_mean)
    group_var = (
        jnp.sum(jnp.where(member & first, centred * centred, 0.0), axis=1, keepdims=True) / GROUP
    )
    group_spread = jnp.maximum(jnp.sqrt(group_var), spread_floor)
    spread_row = jnp.where(valid[:1], spread_over(first, group_spread), 1.0)
    tokens_row = jnp.where(valid[:1], spread_over(~first, sums), 1.0)
    weights = centred / spread_row * (GROUP * WIN / tokens_row)
    products = jnp.where(valid[:1], weights * logprob_sums, 0.0)
    total_rows = GROUPS * GROUP * WIN
    objective_row[...] = -jnp.sum(products, axis=1, keepdims=True) / total_rows
    copies[4].start()

    info_reward, info_group = token_info[1], token_info[2]
    mean, spread, tokens = group_mean[0:1], group_spread[0:1], sums[GROUPS : GROUPS + 1]
    for g in range(1, GROUPS):
        chosen = info_group == float(g)
        mean = jnp.where(chosen, group_mean[g : g + 1], mean)
        spread = jnp.where(chosen, group_spread[g : g + 1], spread)
        tokens = jnp.where(chosen, sums[GROUPS + g : GROUPS + g + 1], tokens)
    info_advantage = (info_reward - mean) / spread
    weight = token_info[0] * (info_advantage * (GROUP * WIN / tokens))
    advantage_row[...] = info_advantage[chunks : chunks + 1, :SUBLANES]
    copies[3].start()
    weight_rows[...] = weight[:chunks]
    copies[2].start()
    for copy in copies:
        copy.wait()


def shards(rewards, group_ids, lengths, token_mask, targets, logits):
    rows = logits.shape[0]
    chunks = rows // LANES
    f32, i32 = jnp.float32, jnp.int32
    any_spec = pl.BlockSpec(memory_space=pl.ANY)

    def kept(shape):
        return pltpu.VMEM(shape, f32)

    def near(array):
        return pltpu.with_memory_space_constraint(array, pltpu.VMEM)

    vmem = pl.BlockSpec(memory_space=pltpu.VMEM)
    stat_shape = (SUBLANES, LANES)
    first_axes = ("mp_0", "mp_2")
    first_size = lax.axis_size("mp_0") * lax.axis_size("mp_2")
    sent, token_info, own_info = pl.pallas_call(
        local_kernel,
        name="local_stats",
        in_specs=[any_spec] * 6,
        out_specs=[vmem] * 3,
        out_shape=[
            kept((first_size, *stat_shape)),
            kept((4, SUBLANES, LANES)),
            kept((SUBLANES, LANES)),
        ],
        scratch_shapes=[
            pltpu.VMEM(logits.shape, logits.dtype),
            pltpu.VMEM((chunks, LANES), i32),
            pltpu.VMEM((chunks, LANES), i32),
            pltpu.SMEM(rewards.shape, i32),
            pltpu.SMEM(rewards.shape, i32),
            pltpu.SMEM(rewards.shape, i32),
            pltpu.SemaphoreType.DMA((chunks + 5,)),
        ],
    )(
        rewards,
        group_ids,
        lengths,
        token_mask.reshape(chunks, LANES),
        targets.reshape(chunks, LANES),
        logits,
    )
    received = lax.all_to_all(sent, first_axes, 0, 0, tiled=True)
    sent = pl.pallas_call(
        merge_kernel,
        name="merge_stats",
        in_specs=[vmem],
        out_specs=vmem,
        out_shape=kept((lax.axis_size("mp_1"), *stat_shape)),
    )(near(received))
    received = lax.all_to_all(sent, "mp_1", 0, 0, tiled=True)
    last_axes = ("dp", "mp_2")
    last_size = lax.axis_size("dp") * lax.axis_size("mp_2")
    sent = pl.pallas_call(
        token_kernel,
        name="token_values",
        in_specs=[vmem] * 3,
        out_specs=vmem,
        out_shape=kept((last_size, *stat_shape)),
    )(near(received), near(token_info), near(own_info))
    received = lax.all_to_all(sent, last_axes, 0, 0, tiled=True)
    advantage, token_weight, token_logprob, token_entropy, objective = pl.pallas_call(
        final_kernel,
        name="group_values",
        in_specs=[vmem] * 2,
        out_specs=[any_spec] * 5,
        out_shape=[
            jax.ShapeDtypeStruct((1, SUBLANES), f32),
            jax.ShapeDtypeStruct((chunks, LANES), f32),
            jax.ShapeDtypeStruct((chunks, LANES), f32),
            jax.ShapeDtypeStruct((chunks, LANES), f32),
            jax.ShapeDtypeStruct((1, 1), f32),
        ],
        scratch_shapes=[
            pltpu.VMEM((1, SUBLANES), f32),
            pltpu.VMEM((chunks, LANES), f32),
            pltpu.VMEM((chunks, LANES), f32),
            pltpu.VMEM((chunks, LANES), f32),
            pltpu.VMEM((1, 1), f32),
            pltpu.SemaphoreType.DMA((5,)),
        ],
    )(near(received), near(token_info))
    return (
        advantage.reshape(-1),
        token_weight.reshape(-1),
        token_logprob.reshape(-1),
        token_entropy.reshape(-1),
        objective.reshape(()),
    )


def solution(mesh):
    split = Mesh(mesh.devices.reshape(mesh.shape["dp"], 8, 8, 2), ("dp", "mp_0", "mp_1", "mp_2"))
    in_specs = (P("dp"), P("dp"), P("dp"), P("dp"), P("dp"), P("dp", MP))
    out_specs = (P("dp"), P("dp"), P("dp"), P("dp"), P())
    return jax.shard_map(
        shards, mesh=split, in_specs=in_specs, out_specs=out_specs, check_vma=False
    )
```

time: 59.5 us -> 60.5 us (1.017)
  blocking collectives: 54.2 us -> 55.6 us
    all_to_all x1, blocking collectives: 13.2 us -> 15.9 us  [shards(): received = lax.all_to_all(sent, last_axes, 0, 0, tiled=True)]
    all_to_all x1, blocking collectives: 26.9 us -> 25.8 us  [shards(): received = lax.all_to_all(sent, first_axes, 0, 0, tiled=True)]
where the time goes in v3:
time: 60.5 us; the launch traced here: 60.3 us
  blocking collectives  55.6 us (92%)
  Pallas kernels  4.03 us (7%)
  between operations  0.65 us (1%)
    all_to_all x1, blocking collectives, shards(): received = lax.all_to_all(sent, first_axes, 0, 0, tiled=True)  25.8 us
    all_to_all x1, blocking collectives, shards(): received = lax.all_to_all(sent, last_axes, 0, 0, tiled=True)  15.9 us
    all_to_all x1, blocking collectives, shards(): received = lax.all_to_all(sent, 'mp_1', 0, 0, tiled=True)  13.9 us
    pallas_call x1, Pallas kernels, shards(): pl.pallas_call(local_kernel, name='local_stats', in_specs=[any_spec] * 6,...  2.86 us

profile of v3, /device:TPU:1, one launch (start us, length us, event | category | flops | bytes accessed | tf_op | source)
XLA Modules:
  0.0 60.3 jit_solution(7965449958097051033)
XLA Ops:
  0.6 2.9 %local_stats.1 = (f32[16,8,128]{2,1,0:T(8,128)S(1)}, f32[4,8,128]{2,1,0:T(8,128)S(1)}, f32[8,128]{1,0:T(8,128)S(1)}) custom-call(s32[8]{0:T(128)} %rewards.1, s32[8]{0:T(128)} %group_ids.1, s32[8]{0:T(128)} %lengths.1, s32[4,128]{1,0:T(4,128)} %bitcast.7, s32[4,128]{1,0:T(4,128)} %bitcast.8, bf16[512,512]{1,0:T(8,128)(2,1)} %logits.1), custom_call_target="tpu_custom_call" | custom-call | tf_op jit(solution)/shard_map/local_stats/pallas_call | solution.py:308
  3.5 25.8 %all_to_all.15.received = f32[16,8,128]{2,1,0:T(8,128)S(1)} all-to-all(f32[16,8,128]{2,1,0:T(8,128)S(1)} %get-tuple-element.13), channel_id=1, replica_groups=mesh['dp'=8,'mp_0'=8,'mp_1'=8,'mp_2'=2] {'mp_0','mp_2'}, dimensions={0} | all-to-all | bytes 131072 | tf_op jit(solution)/shard_map/all_to_all | solution.py:335
  29.3 0.1 merge_stats.1
  29.3 13.9 %all_to_all.16.received = f32[8,8,128]{2,1,0:T(8,128)S(1)} all-to-all(f32[8,8,128]{2,1,0:T(8,128)S(1)} %merge_stats.1), channel_id=1, replica_groups=mesh['dp'=8,'mp_0'=8,'mp_1'=8,'mp_2'=2] {'mp_1'}, dimensions={0} | all-to-all | bytes 65536 | tf_op jit(solution)/shard_map/all_to_all | solution.py:343
  43.3 0.1 token_values.1
  43.4 15.9 %all_to_all.17.received = f32[16,8,128]{2,1,0:T(8,128)S(1)} all-to-all(f32[16,8,128]{2,1,0:T(8,128)S(1)} %token_values.1), channel_id=1, replica_groups=mesh['dp'=8,'mp_0'=8,'mp_1'=8,'mp_2'=2] {'dp','mp_2'}, dimensions={0} | all-to-all | bytes 131072 | tf_op jit(solution)/shard_map/all_to_all | solution.py:353
  59.3 1.0 %group_values.1 = (f32[1,8]{1,0:T(1,128)}, f32[4,128]{1,0:T(4,128)}, f32[4,128]{1,0:T(4,128)}, f32[4,128]{1,0:T(4,128)}, f32[1,1]{1,0:T(1,128)}) custom-call(f32[16,8,128]{2,1,0:T(8,128)S(1)} %all_to_all.17.received, f32[4,8,128]{2,1,0:T(8,128)S(1)} %get-tuple-element.14.token_info), custom_call_target="tpu_custom_call" | custom-call | tf_op jit(solution)/shard_map/group_values/pallas_call | solution.py:354

commit v4 on v2

v4 whole, which is shorter than its diff:
```python
import jax
import jax.numpy as jnp
from jax import lax
from jax.experimental import pallas as pl
from jax.experimental.pallas import tpu as pltpu
from jax.sharding import Mesh
from jax.sharding import PartitionSpec as P

GROUP = 16
WIN = 64
LANES = 128
SUBLANES = 8
GROUPS = 4
STEP = 16
MP = ("mp_0", "mp_1", "mp_2")

spread_floor = 0.25
reward_unit = 1024.0


def lane_of(shape):
    return lax.broadcasted_iota(jnp.int32, shape, 1)


def row_of(shape):
    return lax.broadcasted_iota(jnp.int32, shape, 0)


def lines_to_lanes(pick, block):
    return lax.dot_general(
        pick, block, (((1,), (1,)), ((), ())), preferred_element_type=jnp.float32
    )


def local_kernel(
    rewards, group_ids, lengths, token_mask, targets, logits,
    send, token_info, own_info,
    tiles, target_rows, mask_rows, reward_of, group_of, length_of, peak_rows, columns, sems,
):
    chunks = logits.shape[0] // LANES
    width = logits.shape[1]
    targets_copy = pltpu.make_async_copy(targets, target_rows, sems.at[0])
    small = [
        pltpu.make_async_copy(token_mask, mask_rows, sems.at[1]),
        pltpu.make_async_copy(rewards, reward_of, sems.at[2]),
        pltpu.make_async_copy(group_ids, group_of, sems.at[3]),
        pltpu.make_async_copy(lengths, length_of, sems.at[4]),
    ]
    logits_copy = pltpu.make_async_copy(logits, tiles, sems.at[5])
    targets_copy.start()
    for copy in small:
        copy.start()
    logits_copy.start()
    shard = (
        lax.axis_index("mp_0") * lax.axis_size("mp_1") + lax.axis_index("mp_1")
    ) * lax.axis_size("mp_2") + lax.axis_index("mp_2")
    targets_copy.wait()

    block = (LANES, LANES)
    diagonal = row_of(block) == lane_of(block)
    digit_row = row_of((2 * LANES, LANES))
    digits = jnp.where(digit_row < LANES, 1.0, float(LANES)).astype(jnp.bfloat16)
    local = target_rows[...] - shard * width
    inside = (local >= 0) & (local < width)
    low_digit = jnp.where(inside, local % LANES, -1).astype(jnp.float32)
    high_digit = jnp.where(inside, local // LANES, 0).astype(jnp.float32)
    for c in range(chunks):
        spread = jnp.concatenate(
            [
                jnp.where(diagonal, low_digit[c : c + 1], 0.0),
                jnp.where(diagonal, high_digit[c : c + 1], 0.0),
            ],
            axis=1,
        ).astype(jnp.bfloat16)
        columns[LANES * c : LANES * (c + 1), :] = jnp.dot(
            spread, digits, preferred_element_type=jnp.float32
        )

    for copy in small:
        copy.wait()
    shape = (SUBLANES, LANES)
    row, lane = row_of(shape), lane_of(shape)
    reward_info = jnp.zeros(shape, jnp.float32)
    group_info = jnp.zeros(shape, jnp.float32)
    length_info = jnp.zeros(shape, jnp.int32)
    own = jnp.zeros(shape, jnp.float32)
    for i in range(2 * chunks):
        here = ((row == i // 2) & (lane // WIN == i % 2)) | ((row == chunks) & (lane == i))
        reward = reward_of[i].astype(jnp.float32) / reward_unit
        group = group_of[i].astype(jnp.float32)
        reward_info = jnp.where(here, reward, reward_info)
        group_info = jnp.where(here, group, group_info)
        length_info = jnp.where(here, length_of[i], length_info)
        own = jnp.where(lane == 2 * SUBLANES + i, reward, own)
        own = jnp.where(lane == 3 * SUBLANES + i, group, own)
    mask8 = jnp.concatenate([mask_rows[...], mask_rows[...]], axis=0)
    live = jnp.where((row < chunks) & (mask8 > 0) & (lane % WIN < length_info), 1.0, 0.0)
    token_info[0] = live
    token_info[1] = reward_info
    token_info[2] = group_info
    own_info[...] = own + rollout_sums(live, SUBLANES)

    segments = width // LANES
    step_shape = (STEP, LANES)
    lane_value = lane_of(step_shape).astype(jnp.float32)
    lane_values = [lane_value + float(LANES * k) for k in range(segments)]
    pick_shape = (4 * chunks, 6 * LANES)
    pick_row, pick_lane = row_of(pick_shape), lane_of(pick_shape)
    pick_slot = pick_lane // LANES
    pick_kind = jnp.where(pick_slot < 2, pick_slot, pick_slot // 2 + 1)

    def find_peaks(c):
        for r in range(LANES * c, LANES * (c + 1), STEP):
            best = tiles[r : r + STEP, :LANES]
            for k in range(1, segments):
                best = jnp.maximum(best, tiles[r : r + STEP, LANES * k : LANES * (k + 1)])
            peak_rows[r : r + STEP, :] = jnp.broadcast_to(
                jnp.max(best.astype(jnp.float32), axis=1, keepdims=True), step_shape
            )

    def add_sums(c):
        lines = []
        for r in range(LANES * c, LANES * (c + 1), STEP):
            peak = peak_rows[r : r + STEP, :]
            column = columns[r : r + STEP, :]
            total = moment = picked = 0.0
            for k in range(segments):
                segment = tiles[r : r + STEP, LANES * k : LANES * (k + 1)].astype(jnp.float32)
                shifted = segment - peak
                weight = jnp.exp(shifted)
                product = weight * shifted
                total = weight if k == 0 else total + weight
                moment = product if k == 0 else moment + product
                picked = jnp.where(column == lane_values[k], segment, picked)
            total_high = total.astype(jnp.bfloat16)
            moment_high = moment.astype(jnp.bfloat16)
            lines.append(
                jnp.concatenate(
                    [
                        peak.astype(jnp.bfloat16),
                        picked.astype(jnp.bfloat16),
                        total_high,
                        (total - total_high.astype(jnp.float32)).astype(jnp.bfloat16),
                        moment_high,
                        (moment - moment_high.astype(jnp.float32)).astype(jnp.bfloat16),
                    ],
                    axis=1,
                )
            )
        pick = (pick_row == chunks * pick_kind + c) & ((pick_slot > 0) | (pick_lane == 0))
        return lines_to_lanes(
            jnp.where(pick, 1.0, 0.0).astype(jnp.bfloat16), jnp.concatenate(lines, axis=0)
        )

    logits_copy.wait()
    find_peaks(0)
    gathered = jnp.zeros((4 * chunks, LANES), jnp.float32)
    for c in range(chunks):
        if c + 1 < chunks:
            find_peaks(c + 1)
        gathered += add_sums(c)
    total = gathered[2 * chunks : 3 * chunks]
    log_total = jnp.log(total)
    log_sum = gathered[:chunks] + log_total
    entropy = log_total - gathered[3 * chunks :] / total
    picked = gathered[chunks : 2 * chunks]
    for n in range(send.shape[0]):
        send[n, 0] = log_sum
        send[n, 1] = entropy
        send[n, 2] = picked


def rollout_sums(values, start):
    shape = values.shape
    row, lane = row_of(shape), lane_of(shape)
    even = jnp.sum(jnp.where(lane < WIN, values, 0.0), axis=1, keepdims=True)
    odd = jnp.sum(jnp.where(lane >= WIN, values, 0.0), axis=1, keepdims=True)
    placed = (lane >= start) & (row == (lane - start) // 2)
    spread = jnp.where(placed, jnp.where(lane % 2 == 0, even, odd), 0.0)
    return jnp.broadcast_to(jnp.sum(spread, axis=0, keepdims=True), shape)


def merged(received):
    count = received.shape[0]
    joint = received[0, 0]
    picked = received[0, 2]
    for n in range(1, count):
        joint = jnp.maximum(joint, received[n, 0])
        picked += received[n, 2]
    total = jnp.zeros_like(joint)
    mixed = jnp.zeros_like(joint)
    for n in range(count):
        shift = received[n, 0] - joint
        factor = jnp.exp(shift)
        total += factor
        mixed += factor * (received[n, 1] - shift)
    log_total = jnp.log(total)
    return joint + log_total, mixed / total + log_total, picked


def merge_kernel(received, send):
    log_sum, entropy, picked = merged(received)
    for n in range(send.shape[0]):
        send[n, 0] = log_sum
        send[n, 1] = entropy
        send[n, 2] = picked


def token_kernel(received, token_info, own_info, send, token_values):
    log_sum, entropy, picked = merged(received)
    chunks = log_sum.shape[0]
    live = token_info[0][:chunks]
    logprob = live * (picked - log_sum)
    token_values[:chunks] = logprob
    token_values[chunks:] = live * entropy
    padded = jnp.concatenate([logprob, jnp.zeros_like(logprob)], axis=0)
    send[...] = own_info[...] + rollout_sums(padded, 0)


def final_kernel(
    received, token_info, token_values,
    advantage, token_weight, token_logprob, token_entropy, objective,
    advantage_row, weight_rows, objective_row, sems,
):
    chunks = token_weight.shape[0]
    copies = [
        pltpu.make_async_copy(token_values.at[pl.ds(0, chunks)], token_logprob, sems.at[0]),
        pltpu.make_async_copy(token_values.at[pl.ds(chunks, chunks)], token_entropy, sems.at[1]),
        pltpu.make_async_copy(weight_rows, token_weight, sems.at[2]),
        pltpu.make_async_copy(advantage_row, advantage, sems.at[3]),
        pltpu.make_async_copy(objective_row, objective, sems.at[4]),
    ]
    copies[0].start()
    copies[1].start()
    shape = (SUBLANES, LANES)
    row, lane = row_of(shape), lane_of(shape)
    valid = lane < SUBLANES * received.shape[0]
    shards = pltpu.roll(received[...], 0, 1, stride=SUBLANES, stride_axis=0)

    def field(f):
        shifted = pltpu.roll(shards, LANES - SUBLANES * f, 1) if f else shards
        return jnp.sum(
            jnp.where(lane // SUBLANES == row, shifted, 0.0), axis=0, keepdims=True
        )

    logprob_sums, counts, reward_values, groups = (field(f) for f in range(4))
    first = row < GROUPS
    member = (groups == (row % GROUPS).astype(jnp.float32)) & valid
    sums = jnp.sum(
        jnp.where(member, jnp.where(first, reward_values, counts), 0.0), axis=1, keepdims=True
    )
    group_mean = sums / GROUP

    def spread_over(chosen, values):
        return jnp.sum(jnp.where(member & chosen, values, 0.0), axis=0, keepdims=True)

    centred = reward_values - spread_over(first, group_mean)
    group_var = (
        jnp.sum(jnp.where(member & first, centred * centred, 0.0), axis=1, keepdims=True) / GROUP
    )
    group_spread = jnp.maximum(jnp.sqrt(group_var), spread_floor)

    info_reward, info_group = token_info[1], token_info[2]
    mean, spread, tokens = group_mean[0:1], group_spread[0:1], sums[GROUPS : GROUPS + 1]
    for g in range(1, GROUPS):
        chosen = info_group == float(g)
        mean = jnp.where(chosen, group_mean[g : g + 1], mean)
        spread = jnp.where(chosen, group_spread[g : g + 1], spread)
        tokens = jnp.where(chosen, sums[GROUPS + g : GROUPS + g + 1], tokens)
    info_advantage = (info_reward - mean) / spread
    weight = token_info[0] * (info_advantage * (GROUP * WIN / tokens))
    advantage_row[...] = info_advantage[chunks : chunks + 1, :SUBLANES]
    copies[3].start()
    weight_rows[...] = weight[:chunks]
    copies[2].start()

    spread_row = jnp.where(valid[:1], spread_over(first, group_spread), 1.0)
    tokens_row = jnp.where(valid[:1], spread_over(~first, sums), 1.0)
    weights = centred / spread_row * (GROUP * WIN / tokens_row)
    products = jnp.where(valid[:1], weights * logprob_sums, 0.0)
    total_rows = GROUPS * GROUP * WIN
    objective_row[...] = -jnp.sum(products, axis=1, keepdims=True) / total_rows
    copies[4].start()
    for copy in copies:
        copy.wait()


def shards(rewards, group_ids, lengths, token_mask, targets, logits):
    rows = logits.shape[0]
    chunks = rows // LANES
    f32, i32 = jnp.float32, jnp.int32
    any_spec = pl.BlockSpec(memory_space=pl.ANY)
    vmem = pl.BlockSpec(memory_space=pltpu.VMEM)

    def kept(*shape):
        return pltpu.VMEM(shape, f32)

    def near(array):
        return pltpu.with_memory_space_constraint(array, pltpu.VMEM)

    first_axes = ("mp_0", "mp_2")
    first_size = lax.axis_size("mp_0") * lax.axis_size("mp_2")
    sent, token_info, own_info = pl.pallas_call(
        local_kernel,
        name="local_stats",
        in_specs=[any_spec] * 6,
        out_specs=[vmem] * 3,
        out_shape=[
            kept(first_size, 3, chunks, LANES),
            kept(3, SUBLANES, LANES),
            kept(SUBLANES, LANES),
        ],
        scratch_shapes=[
            pltpu.VMEM(logits.shape, logits.dtype),
            pltpu.VMEM((chunks, LANES), i32),
            pltpu.VMEM((chunks, LANES), i32),
            pltpu.SMEM(rewards.shape, i32),
            pltpu.SMEM(rewards.shape, i32),
            pltpu.SMEM(rewards.shape, i32),
            pltpu.VMEM((rows, LANES), f32),
            pltpu.VMEM((rows, LANES), f32),
            pltpu.SemaphoreType.DMA((6,)),
        ],
    )(
        rewards,
        group_ids,
        lengths,
        token_mask.reshape(chunks, LANES),
        targets.reshape(chunks, LANES),
        logits,
    )
    received = lax.all_to_all(sent, first_axes, 0, 0, tiled=True)
    sent = pl.pallas_call(
        merge_kernel,
        name="merge_stats",
        in_specs=[vmem],
        out_specs=vmem,
        out_shape=kept(lax.axis_size("mp_1"), 3, chunks, LANES),
    )(near(received))
    received = lax.all_to_all(sent, "mp_1", 0, 0, tiled=True)
    shard_count = lax.axis_size("dp")
    sent, token_values = pl.pallas_call(
        token_kernel,
        name="token_values",
        in_specs=[vmem] * 3,
        out_specs=[vmem] * 2,
        out_shape=[kept(SUBLANES, LANES), kept(2 * chunks, LANES)],
    )(near(received), near(token_info), near(own_info))
    received = lax.all_to_all(sent.reshape(shard_count, 1, LANES), "dp", 0, 0, tiled=True)
    advantage, token_weight, token_logprob, token_entropy, objective = pl.pallas_call(
        final_kernel,
        name="group_values",
        in_specs=[vmem] * 3,
        out_specs=[any_spec] * 5,
        out_shape=[
            jax.ShapeDtypeStruct((1, SUBLANES), f32),
            jax.ShapeDtypeStruct((chunks, LANES), f32),
            jax.ShapeDtypeStruct((chunks, LANES), f32),
            jax.ShapeDtypeStruct((chunks, LANES), f32),
            jax.ShapeDtypeStruct((1, 1), f32),
        ],
        scratch_shapes=[
            pltpu.VMEM((1, SUBLANES), f32),
            pltpu.VMEM((chunks, LANES), f32),
            pltpu.VMEM((1, 1), f32),
            pltpu.SemaphoreType.DMA((5,)),
        ],
    )(near(received.reshape(shard_count, LANES)), near(token_info), near(token_values))
    return (
        advantage.reshape(-1),
        token_weight.reshape(-1),
        token_logprob.reshape(-1),
        token_entropy.reshape(-1),
        objective.reshape(()),
    )


def solution(mesh):
    split = Mesh(mesh.devices.reshape(mesh.shape["dp"], 8, 8, 2), ("dp", "mp_0", "mp_1", "mp_2"))
    in_specs = (P("dp"), P("dp"), P("dp"), P("dp"), P("dp"), P("dp", MP))
    out_specs = (P("dp"), P("dp"), P("dp"), P("dp"), P())
    return jax.shard_map(
        shards, mesh=split, in_specs=in_specs, out_specs=out_specs, check_vma=False
    )
```

time: 59.5 us -> 57.6 us (0.968)
  Pallas kernels: 3.9 us -> 2.89 us
  blocking collectives: 54.2 us -> 53.3 us
    pallas_call x1, Pallas kernels: 2.76 us -> 1.77 us  [shards(): pl.pallas_call(local_kernel, name='local_stats', in_specs=[any_spec] * 6,...]
where the time goes in v4:
time: 57.6 us; the launch traced here: 56.9 us
  blocking collectives  53.3 us (93%)
  Pallas kernels  2.89 us (5%)
  between operations  0.64 us (1%)
    all_to_all x1, blocking collectives, shards(): received = lax.all_to_all(sent, first_axes, 0, 0, tiled=True)  26.4 us
    all_to_all x1, blocking collectives, shards(): received = lax.all_to_all(sent, 'mp_1', 0, 0, tiled=True)  14.1 us
    all_to_all x1, blocking collectives, shards(): lax.all_to_all(sent.reshape(shard_count, 1, LANES), 'dp', 0, 0, tiled=True)  12.8 us
    pallas_call x1, Pallas kernels, shards(): pl.pallas_call(local_kernel, name='local_stats', in_specs=[any_spec] * 6,...  1.77 us

profile of v4, /device:TPU:1, one launch (start us, length us, event | category | flops | bytes accessed | tf_op | source)
XLA Modules:
  0.0 56.9 jit_solution(13783201611832991805)
XLA Ops:
  0.6 1.8 %local_stats.1 = (f32[16,3,4,128]{3,2,1,0:T(4,128)S(1)}, f32[3,8,128]{2,1,0:T(8,128)S(1)}, f32[8,128]{1,0:T(8,128)S(1)}) custom-call(s32[8]{0:T(128)} %rewards.1, s32[8]{0:T(128)} %group_ids.1, s32[8]{0:T(128)} %lengths.1, s32[4,128]{1,0:T(4,128)} %bitcast.13, s32[4,128]{1,0:T(4,128)} %bitcast.14, bf16[512,512]{1,0:T(8,128)(2,1)} %logits.1), custom_call_target="tpu_custom_call" | custom-call | tf_op jit(solution)/shard_map/local_stats/pallas_call | solution.py:303
  2.4 26.4 %all_to_all.15.received = f32[16,3,4,128]{3,2,1,0:T(4,128)S(1)} all-to-all(f32[16,3,4,128]{3,2,1,0:T(4,128)S(1)} %get-tuple-element.15), channel_id=1, replica_groups=mesh['dp'=8,'mp_0'=8,'mp_1'=8,'mp_2'=2] {'mp_0','mp_2'}, dimensions={0} | all-to-all | bytes 196608 | tf_op jit(solution)/shard_map/all_to_all | solution.py:332
  28.9 14.1 %all_to_all.16.received = f32[8,3,4,128]{3,2,1,0:T(4,128)S(1)} all-to-all(f32[8,3,4,128]{3,2,1,0:T(4,128)S(1)} %merge_stats.1), channel_id=1, replica_groups=mesh['dp'=8,'mp_0'=8,'mp_1'=8,'mp_2'=2] {'mp_1'}, dimensions={0} | all-to-all | bytes 98304 | tf_op jit(solution)/shard_map/all_to_all | solution.py:340
  43.0 0.1 token_values.1
  43.1 12.8 %all_to_all.17 = f32[8,1,128]{2,1,0:T(1,128)S(1)} all-to-all(f32[8,1,128]{2,1,0:T(1,128)S(1)} %bitcast.12), channel_id=1, replica_groups=mesh['dp'=8,'mp_0'=8,'mp_1'=8,'mp_2'=2] {'dp'}, dimensions={0} | all-to-all | bytes 8192 | tf_op jit(solution)/shard_map/all_to_all | solution.py:349
  55.9 1.0 %group_values.1 = (f32[1,8]{1,0:T(1,128)}, f32[4,128]{1,0:T(4,128)}, f32[4,128]{1,0:T(4,128)}, f32[4,128]{1,0:T(4,128)}, f32[1,1]{1,0:T(1,128)}) custom-call(f32[8,128]{1,0:T(8,128)S(1)} %bitcast.11, f32[3,8,128]{2,1,0:T(8,128)S(1)} %get-tuple-element.16.token_info, f32[8,128]{1,0:T(8,128)S(1)} %get-tuple-element.19.token_values), custom_call_target="tpu_custom_call" | custom-call | tf_op jit(solution)/shard_map/group_values/pallas_call | solution.py:350
  (1 shorter events, 0.0 us)

commit v5 on v4

--- a/solution.py
+++ b/solution.py
@@ -83,22 +83,29 @@
     reward_info = jnp.zeros(shape, jnp.float32)
     group_info = jnp.zeros(shape, jnp.float32)
     length_info = jnp.zeros(shape, jnp.int32)
-    own = jnp.zeros(shape, jnp.float32)
+    own_reward = jnp.zeros(shape, jnp.float32)
+    own_group = jnp.zeros(shape, jnp.int32)
     for i in range(2 * chunks):
         here = ((row == i // 2) & (lane // WIN == i % 2)) | ((row == chunks) & (lane == i))
         reward = reward_of[i].astype(jnp.float32) / reward_unit
-        group = group_of[i].astype(jnp.float32)
         reward_info = jnp.where(here, reward, reward_info)
-        group_info = jnp.where(here, group, group_info)
+        group_info = jnp.where(here, group_of[i].astype(jnp.float32), group_info)
         length_info = jnp.where(here, length_of[i], length_info)
-        own = jnp.where(lane == 2 * SUBLANES + i, reward, own)
-        own = jnp.where(lane == 3 * SUBLANES + i, group, own)
+        own_reward = jnp.where(lane % SUBLANES == i, reward, own_reward)
+        own_group = jnp.where(lane % SUBLANES == i, group_of[i], own_group)
     mask8 = jnp.concatenate([mask_rows[...], mask_rows[...]], axis=0)
     live = jnp.where((row < chunks) & (mask8 > 0) & (lane % WIN < length_info), 1.0, 0.0)
     token_info[0] = live
     token_info[1] = reward_info
     token_info[2] = group_info
-    own_info[...] = own + rollout_sums(live, SUBLANES)
+    slot = lane // SUBLANES
+    field = slot // GROUPS
+    values = jnp.where(
+        field == 0, own_reward, jnp.where(field == 1, rollout_sums(live), 1.0)
+    )
+    mine = own_group == slot % GROUPS
+    own_info[0] = jnp.where(mine & (field != 2), values, 0.0)
+    own_info[1] = jnp.where(mine & (field == 2), 1.0, 0.0)
 
     segments = width // LANES
     step_shape = (STEP, LANES)
@@ -170,13 +177,14 @@
         send[n, 2] = picked
 
 
-def rollout_sums(values, start):
+def rollout_sums(values):
     shape = values.shape
     row, lane = row_of(shape), lane_of(shape)
     even = jnp.sum(jnp.where(lane < WIN, values, 0.0), axis=1, keepdims=True)
     odd = jnp.sum(jnp.where(lane >= WIN, values, 0.0), axis=1, keepdims=True)
-    placed = (lane >= start) & (row == (lane - start) // 2)
-    spread = jnp.where(placed, jnp.where(lane % 2 == 0, even, odd), 0.0)
+    spread = jnp.where(
+        row == lane % SUBLANES // 2, jnp.where(lane % 2 == 0, even, odd), 0.0
+    )
     return jnp.broadcast_to(jnp.sum(spread, axis=0, keepdims=True), shape)
 
 
@@ -214,7 +222,7 @@
     token_values[:chunks] = logprob
     token_values[chunks:] = live * entropy
     padded = jnp.concatenate([logprob, jnp.zeros_like(logprob)], axis=0)
-    send[...] = own_info[...] + rollout_sums(padded, 0)
+    send[...] = own_info[0] + own_info[1] * rollout_sums(padded)
 
 
 def final_kernel(
@@ -234,53 +242,48 @@
     copies[1].start()
     shape = (SUBLANES, LANES)
     row, lane = row_of(shape), lane_of(shape)
-    valid = lane < SUBLANES * received.shape[0]
-    shards = pltpu.roll(received[...], 0, 1, stride=SUBLANES, stride_axis=0)
-
-    def field(f):
-        shifted = pltpu.roll(shards, LANES - SUBLANES * f, 1) if f else shards
-        return jnp.sum(
-            jnp.where(lane // SUBLANES == row, shifted, 0.0), axis=0, keepdims=True
+    slot = lane // SUBLANES
+    first = row < GROUPS
+    own_slot = slot == row
+    rewards = received[...]
+    logprob_sums = pltpu.roll(rewards, LANES // 2, 1)
+    member = pltpu.roll(rewards, LANES // 4, 1)
+
+    def row_sums(upper, lower):
+        upper = jnp.sum(upper, axis=0, keepdims=True)
+        lower = jnp.sum(lower, axis=0, keepdims=True)
+        chosen = jnp.where(
+            first, jnp.where(own_slot, upper, 0.0), jnp.where(slot == row - GROUPS, lower, 0.0)
         )
-
-    logprob_sums, counts, reward_values, groups = (field(f) for f in range(4))
-    first = row < GROUPS
-    member = (groups == (row % GROUPS).astype(jnp.float32)) & valid
-    sums = jnp.sum(
-        jnp.where(member, jnp.where(first, reward_values, counts), 0.0), axis=1, keepdims=True
-    )
+        return jnp.sum(chosen, axis=1, keepdims=True)
+
+    total = jnp.sum(rewards, axis=0, keepdims=True)
+    sums = jnp.sum(jnp.where(own_slot, total, 0.0), axis=1, keepdims=True)
     group_mean = sums / GROUP
-
-    def spread_over(chosen, values):
-        return jnp.sum(jnp.where(member & chosen, values, 0.0), axis=0, keepdims=True)
-
-    centred = reward_values - spread_over(first, group_mean)
-    group_var = (
-        jnp.sum(jnp.where(member & first, centred * centred, 0.0), axis=1, keepdims=True) / GROUP
-    )
-    group_spread = jnp.maximum(jnp.sqrt(group_var), spread_floor)
-
+    mean_row = jnp.sum(jnp.where(own_slot & first, group_mean, 0.0), axis=0, keepdims=True)
+    centred = rewards - member * mean_row
+    spreads = row_sums(centred * centred, centred * logprob_sums)
+    group_spread = jnp.maximum(jnp.sqrt(spreads / GROUP), spread_floor)
     info_reward, info_group = token_info[1], token_info[2]
     mean, spread, tokens = group_mean[0:1], group_spread[0:1], sums[GROUPS : GROUPS + 1]
+    terms = spreads[GROUPS : GROUPS + 1] * (GROUP * WIN / tokens) / spread
     for g in range(1, GROUPS):
         chosen = info_group == float(g)
+        one_tokens = sums[GROUPS + g : GROUPS + g + 1]
+        one_spread = group_spread[g : g + 1]
+        terms += spreads[GROUPS + g : GROUPS + g + 1] * (GROUP * WIN / one_tokens) / one_spread
         mean = jnp.where(chosen, group_mean[g : g + 1], mean)
-        spread = jnp.where(chosen, group_spread[g : g + 1], spread)
-        tokens = jnp.where(chosen, sums[GROUPS + g : GROUPS + g + 1], tokens)
+        spread = jnp.where(chosen, one_spread, spread)
+        tokens = jnp.where(chosen, one_tokens, tokens)
+    total_rows = GROUPS * GROUP * WIN
+    objective_row[...] = -terms / total_rows
+    copies[4].start()
     info_advantage = (info_reward - mean) / spread
     weight = token_info[0] * (info_advantage * (GROUP * WIN / tokens))
     advantage_row[...] = info_advantage[chunks : chunks + 1, :SUBLANES]
     copies[3].start()
     weight_rows[...] = weight[:chunks]
     copies[2].start()
-
-    spread_row = jnp.where(valid[:1], spread_over(first, group_spread), 1.0)
-    tokens_row = jnp.where(valid[:1], spread_over(~first, sums), 1.0)
-    weights = centred / spread_row * (GROUP * WIN / tokens_row)
-    products = jnp.where(valid[:1], weights * logprob_sums, 0.0)
-    total_rows = GROUPS * GROUP * WIN
-    objective_row[...] = -jnp.sum(products, axis=1, keepdims=True) / total_rows
-    copies[4].start()
     for copy in copies:
         copy.wait()
 
@@ -298,8 +301,8 @@
     def near(array):
         return pltpu.with_memory_space_constraint(array, pltpu.VMEM)
 
-    first_axes = ("mp_0", "mp_2")
-    first_size = lax.axis_size("mp_0") * lax.axis_size("mp_2")
+    first_axes = ("mp_1", "mp_2")
+    first_size = lax.axis_size("mp_1") * lax.axis_size("mp_2")
     sent, token_info, own_info = pl.pallas_call(
         local_kernel,
         name="local_stats",
@@ -308,7 +311,7 @@
         out_shape=[
             kept(first_size, 3, chunks, LANES),
             kept(3, SUBLANES, LANES),
-            kept(SUBLANES, LANES),
+            kept(2, SUBLANES, LANES),
         ],
         scratch_shapes=[
             pltpu.VMEM(logits.shape, logits.dtype),
@@ -335,9 +338,9 @@
         name="merge_stats",
         in_specs=[vmem],
         out_specs=vmem,
-        out_shape=kept(lax.axis_size("mp_1"), 3, chunks, LANES),
+        out_shape=kept(lax.axis_size("mp_0"), 3, chunks, LANES),
     )(near(received))
-    received = lax.all_to_all(sent, "mp_1", 0, 0, tiled=True)
+    received = lax.all_to_all(sent, "mp_0", 0, 0, tiled=True)
     shard_count = lax.axis_size("dp")
     sent, token_values = pl.pallas_call(
         token_kernel,

time: 57.6 us -> 57.5 us (level)
    all_to_all x1, blocking collectives: 14.1 us -> 15.5 us  [shards(): received = lax.all_to_all(sent, 'mp_0', 0, 0, tiled=True)]
    all_to_all x1, blocking collectives: 26.4 us -> 25 us  [shards(): received = lax.all_to_all(sent, first_axes, 0, 0, tiled=True)]
where the time goes in v5:
time: 57.5 us; the launch traced here: 56.8 us
  blocking collectives  53.4 us (93%)
  Pallas kernels  2.76 us (5%)
  between operations  0.64 us (1%)
    all_to_all x1, blocking collectives, shards(): received = lax.all_to_all(sent, first_axes, 0, 0, tiled=True)  25 us
    all_to_all x1, blocking collectives, shards(): received = lax.all_to_all(sent, 'mp_0', 0, 0, tiled=True)  15.5 us
    all_to_all x1, blocking collectives, shards(): lax.all_to_all(sent.reshape(shard_count, 1, LANES), 'dp', 0, 0, tiled=True)  12.9 us
    pallas_call x1, Pallas kernels, shards(): pl.pallas_call(local_kernel, name='local_stats', in_specs=[any_spec] * 6,...  1.77 us

profile of v5, /device:TPU:1, one launch (start us, length us, event | category | flops | bytes accessed | tf_op | source)
XLA Modules:
  0.0 56.8 jit_solution(14486250423545930820)
XLA Ops:
  0.6 1.8 %local_stats.1 = (f32[16,3,4,128]{3,2,1,0:T(4,128)S(1)}, f32[3,8,128]{2,1,0:T(8,128)S(1)}, f32[2,8,128]{2,1,0:T(8,128)S(1)}) custom-call(s32[8]{0:T(128)} %rewards.1, s32[8]{0:T(128)} %group_ids.1, s32[8]{0:T(128)} %lengths.1, s32[4,128]{1,0:T(4,128)} %bitcast.13, s32[4,128]{1,0:T(4,128)} %bitcast.14, bf16[512,512]{1,0:T(8,128)(2,1)} %logits.1), custom_call_target="tpu_custom_call" | custom-call | tf_op jit(solution)/shard_map/local_stats/pallas_call | solution.py:306
  2.4 25.0 %all_to_all.15.received = f32[16,3,4,128]{3,2,1,0:T(4,128)S(1)} all-to-all(f32[16,3,4,128]{3,2,1,0:T(4,128)S(1)} %get-tuple-element.15), channel_id=1, replica_groups=mesh['dp'=8,'mp_0'=8,'mp_1'=8,'mp_2'=2] {'mp_1','mp_2'}, dimensions={0} | all-to-all | bytes 196608 | tf_op jit(solution)/shard_map/all_to_all | solution.py:335
  27.5 15.5 %all_to_all.16.received = f32[8,3,4,128]{3,2,1,0:T(4,128)S(1)} all-to-all(f32[8,3,4,128]{3,2,1,0:T(4,128)S(1)} %merge_stats.1), channel_id=1, replica_groups=mesh['dp'=8,'mp_0'=8,'mp_1'=8,'mp_2'=2] {'mp_0'}, dimensions={0} | all-to-all | bytes 98304 | tf_op jit(solution)/shard_map/all_to_all | solution.py:343
  43.0 0.1 token_values.1
  43.1 12.9 %all_to_all.17 = f32[8,1,128]{2,1,0:T(1,128)S(1)} all-to-all(f32[8,1,128]{2,1,0:T(1,128)S(1)} %bitcast.12), channel_id=1, replica_groups=mesh['dp'=8,'mp_0'=8,'mp_1'=8,'mp_2'=2] {'dp'}, dimensions={0} | all-to-all | bytes 8192 | tf_op jit(solution)/shard_map/all_to_all | solution.py:352
  55.9 0.8 %group_values.1 = (f32[1,8]{1,0:T(1,128)}, f32[4,128]{1,0:T(4,128)}, f32[4,128]{1,0:T(4,128)}, f32[4,128]{1,0:T(4,128)}, f32[1,1]{1,0:T(1,128)}) custom-call(f32[8,128]{1,0:T(8,128)S(1)} %bitcast.11, f32[3,8,128]{2,1,0:T(8,128)S(1)} %get-tuple-element.16.token_info, f32[8,128]{1,0:T(8,128)S(1)} %get-tuple-element.19.token_values), custom_call_target="tpu_custom_call" | custom-call | tf_op jit(solution)/shard_map/group_values/pallas_call | solution.py:353
  (1 shorter events, 0.0 us)

commit v6 on v5

--- a/solution.py
+++ b/solution.py
@@ -301,8 +301,8 @@
     def near(array):
         return pltpu.with_memory_space_constraint(array, pltpu.VMEM)
 
-    first_axes = ("mp_1", "mp_2")
-    first_size = lax.axis_size("mp_1") * lax.axis_size("mp_2")
+    first_axes = ("mp_2", "mp_0")
+    first_size = lax.axis_size("mp_2") * lax.axis_size("mp_0")
     sent, token_info, own_info = pl.pallas_call(
         local_kernel,
         name="local_stats",
@@ -338,9 +338,9 @@
         name="merge_stats",
         in_specs=[vmem],
         out_specs=vmem,
-        out_shape=kept(lax.axis_size("mp_0"), 3, chunks, LANES),
+        out_shape=kept(lax.axis_size("mp_1"), 3, chunks, LANES),
     )(near(received))
-    received = lax.all_to_all(sent, "mp_0", 0, 0, tiled=True)
+    received = lax.all_to_all(sent, "mp_1", 0, 0, tiled=True)
     shard_count = lax.axis_size("dp")
     sent, token_values = pl.pallas_call(
         token_kernel,

time: 57.5 us -> 57.5 us (level)
  the two profiles are of different devices: /device:TPU:1 before, /device:TPU:2 now
where the time goes in v6:
time: 57.5 us; the launch traced here: 57.2 us
  blocking collectives  53.8 us (94%)
  Pallas kernels  2.76 us (5%)
  between operations  0.64 us (1%)
    all_to_all x1, blocking collectives, shards(): received = lax.all_to_all(sent, first_axes, 0, 0, tiled=True)  24.9 us
    all_to_all x1, blocking collectives, shards(): received = lax.all_to_all(sent, 'mp_1', 0, 0, tiled=True)  15.6 us
    all_to_all x1, blocking collectives, shards(): lax.all_to_all(sent.reshape(shard_count, 1, LANES), 'dp', 0, 0, tiled=True)  13.3 us
    pallas_call x1, Pallas kernels, shards(): pl.pallas_call(local_kernel, name='local_stats', in_specs=[any_spec] * 6,...  1.77 us

profile of v6, /device:TPU:2, one launch (start us, length us, event | category | flops | bytes accessed | tf_op | source)
XLA Modules:
  0.0 57.2 jit_solution(14008156317324618616)
XLA Ops:
  0.6 1.8 %local_stats.1 = (f32[16,3,4,128]{3,2,1,0:T(4,128)S(1)}, f32[3,8,128]{2,1,0:T(8,128)S(1)}, f32[2,8,128]{2,1,0:T(8,128)S(1)}) custom-call(s32[8]{0:T(128)} %rewards.1, s32[8]{0:T(128)} %group_ids.1, s32[8]{0:T(128)} %lengths.1, s32[4,128]{1,0:T(4,128)} %bitcast.13, s32[4,128]{1,0:T(4,128)} %bitcast.14, bf16[512,512]{1,0:T(8,128)(2,1)} %logits.1), custom_call_target="tpu_custom_call" | custom-call | tf_op jit(solution)/shard_map/local_stats/pallas_call | solution.py:306
  2.4 24.9 %all_to_all.15.received = f32[16,3,4,128]{3,2,1,0:T(4,128)S(1)} all-to-all(f32[16,3,4,128]{3,2,1,0:T(4,128)S(1)} %get-tuple-element.15), channel_id=1, replica_groups=mesh['dp'=8,'mp_0'=8,'mp_1'=8,'mp_2'=2] {'mp_2','mp_0'}, dimensions={0} | all-to-all | bytes 196608 | tf_op jit(solution)/shard_map/all_to_all | solution.py:335
  27.4 15.6 %all_to_all.16.received = f32[8,3,4,128]{3,2,1,0:T(4,128)S(1)} all-to-all(f32[8,3,4,128]{3,2,1,0:T(4,128)S(1)} %merge_stats.1), channel_id=1, replica_groups=mesh['dp'=8,'mp_0'=8,'mp_1'=8,'mp_2'=2] {'mp_1'}, dimensions={0} | all-to-all | bytes 98304 | tf_op jit(solution)/shard_map/all_to_all | solution.py:343
  42.9 0.1 token_values.1
  43.0 13.3 %all_to_all.17 = f32[8,1,128]{2,1,0:T(1,128)S(1)} all-to-all(f32[8,1,128]{2,1,0:T(1,128)S(1)} %bitcast.12), channel_id=1, replica_groups=mesh['dp'=8,'mp_0'=8,'mp_1'=8,'mp_2'=2] {'dp'}, dimensions={0} | all-to-all | bytes 8192 | tf_op jit(solution)/shard_map/all_to_all | solution.py:352
  56.4 0.8 %group_values.1 = (f32[1,8]{1,0:T(1,128)}, f32[4,128]{1,0:T(4,128)}, f32[4,128]{1,0:T(4,128)}, f32[4,128]{1,0:T(4,128)}, f32[1,1]{1,0:T(1,128)}) custom-call(f32[8,128]{1,0:T(8,128)S(1)} %bitcast.11, f32[3,8,128]{2,1,0:T(8,128)S(1)} %get-tuple-element.16.token_info, f32[8,128]{1,0:T(8,128)S(1)} %get-tuple-element.19.token_values), custom_call_target="tpu_custom_call" | custom-call | tf_op jit(solution)/shard_map/group_values/pallas_call | solution.py:353
  (1 shorter events, 0.0 us)

commit v7 on v6

--- a/solution.py
+++ b/solution.py
@@ -12,7 +12,13 @@
 SUBLANES = 8
 GROUPS = 4
 STEP = 16
-MP = ("mp_0", "mp_1", "mp_2")
+X_AXES = ("x2", "x1", "x0")
+Z_AXES = ("z2", "z1", "z0")
+Y_AXES = ("y2", "y1", "y0")
+MP = Z_AXES + Y_AXES + ("core",)
+FIRST = ("z0", "z1", "z2", "core")
+SECOND = ("y0", "y1", "y2")
+THIRD = ("x0", "x1", "x2")
 
 spread_floor = 0.25
 reward_unit = 1024.0
@@ -51,9 +57,9 @@
     for copy in small:
         copy.start()
     logits_copy.start()
-    shard = (
-        lax.axis_index("mp_0") * lax.axis_size("mp_1") + lax.axis_index("mp_1")
-    ) * lax.axis_size("mp_2") + lax.axis_index("mp_2")
+    shard = 0
+    for name in MP:
+        shard = shard * 2 + lax.axis_index(name)
     targets_copy.wait()
 
     block = (LANES, LANES)
@@ -301,15 +307,13 @@
     def near(array):
         return pltpu.with_memory_space_constraint(array, pltpu.VMEM)
 
-    first_axes = ("mp_2", "mp_0")
-    first_size = lax.axis_size("mp_2") * lax.axis_size("mp_0")
     sent, token_info, own_info = pl.pallas_call(
         local_kernel,
         name="local_stats",
         in_specs=[any_spec] * 6,
         out_specs=[vmem] * 3,
         out_shape=[
-            kept(first_size, 3, chunks, LANES),
+            kept(2 ** len(FIRST), 3, chunks, LANES),
             kept(3, SUBLANES, LANES),
             kept(2, SUBLANES, LANES),
         ],
@@ -332,16 +336,16 @@
         targets.reshape(chunks, LANES),
         logits,
     )
-    received = lax.all_to_all(sent, first_axes, 0, 0, tiled=True)
+    received = lax.all_to_all(sent, FIRST, 0, 0, tiled=True)
     sent = pl.pallas_call(
         merge_kernel,
         name="merge_stats",
         in_specs=[vmem],
         out_specs=vmem,
-        out_shape=kept(lax.axis_size("mp_1"), 3, chunks, LANES),
+        out_shape=kept(2 ** len(SECOND), 3, chunks, LANES),
     )(near(received))
-    received = lax.all_to_all(sent, "mp_1", 0, 0, tiled=True)
-    shard_count = lax.axis_size("dp")
+    received = lax.all_to_all(sent, SECOND, 0, 0, tiled=True)
+    shard_count = 2 ** len(THIRD)
     sent, token_values = pl.pallas_call(
         token_kernel,
         name="token_values",
@@ -349,7 +353,7 @@
         out_specs=[vmem] * 2,
         out_shape=[kept(SUBLANES, LANES), kept(2 * chunks, LANES)],
     )(near(received), near(token_info), near(own_info))
-    received = lax.all_to_all(sent.reshape(shard_count, 1, LANES), "dp", 0, 0, tiled=True)
+    received = lax.all_to_all(sent.reshape(shard_count, 1, LANES), THIRD, 0, 0, tiled=True)
     advantage, token_weight, token_logprob, token_entropy, objective = pl.pallas_call(
         final_kernel,
         name="group_values",
@@ -379,9 +383,11 @@
 
 
 def solution(mesh):
-    split = Mesh(mesh.devices.reshape(mesh.shape["dp"], 8, 8, 2), ("dp", "mp_0", "mp_1", "mp_2"))
-    in_specs = (P("dp"), P("dp"), P("dp"), P("dp"), P("dp"), P("dp", MP))
-    out_specs = (P("dp"), P("dp"), P("dp"), P("dp"), P())
+    names = X_AXES + MP
+    split = Mesh(mesh.devices.reshape((2,) * len(names)), names)
+    rows = P(X_AXES)
+    in_specs = (rows, rows, rows, rows, rows, P(X_AXES, MP))
+    out_specs = (rows, rows, rows, rows, P())
     return jax.shard_map(
         shards, mesh=split, in_specs=in_specs, out_specs=out_specs, check_vma=False
     )

time: 57.5 us -> 57.1 us (level)
  the two profiles are of different devices: /device:TPU:2 before, /device:TPU:1 now
where the time goes in v7:
time: 57.1 us; the launch traced here: 56.4 us
  blocking collectives  53 us (93%)
  Pallas kernels  2.76 us (5%)
  between operations  0.64 us (1%)
    all_to_all x1, blocking collectives, shards(): received = lax.all_to_all(sent, FIRST, 0, 0, tiled=True)  26.4 us
    all_to_all x1, blocking collectives, shards(): received = lax.all_to_all(sent, SECOND, 0, 0, tiled=True)  13.8 us
    all_to_all x1, blocking collectives, shards(): lax.all_to_all(sent.reshape(shard_count, 1, LANES), THIRD, 0, 0, tiled=True)  12.8 us
    pallas_call x1, Pallas kernels, shards(): pl.pallas_call(local_kernel, name='local_stats', in_specs=[any_spec] * 6,...  1.77 us

profile of v7, /device:TPU:1, one launch (start us, length us, event | category | flops | bytes accessed | tf_op | source)
XLA Modules:
  0.0 56.4 jit_solution(2177994398590672922)
XLA Ops:
  0.6 1.8 %local_stats.1 = (f32[16,3,4,128]{3,2,1,0:T(4,128)S(1)}, f32[3,8,128]{2,1,0:T(8,128)S(1)}, f32[2,8,128]{2,1,0:T(8,128)S(1)}) custom-call(s32[8]{0:T(128)} %rewards.1, s32[8]{0:T(128)} %group_ids.1, s32[8]{0:T(128)} %lengths.1, s32[4,128]{1,0:T(4,128)} %bitcast.13, s32[4,128]{1,0:T(4,128)} %bitcast.14, bf16[512,512]{1,0:T(8,128)(2,1)} %logits.1), custom_call_target="tpu_custom_call" | custom-call | tf_op jit(solution)/shard_map/local_stats/pallas_call | solution.py:310
  2.4 26.4 %all_to_all.15.received = f32[16,3,4,128]{3,2,1,0:T(4,128)S(1)} all-to-all(f32[16,3,4,128]{3,2,1,0:T(4,128)S(1)} %get-tuple-element.15), channel_id=1, replica_groups=mesh['x2'=2,'x1'=2,'x0'=2,'z2'=2,'z1'=2,'z0'=2,'y2'=2,'y1'=2,'y0'=2,'cor..., dimensions={0} | all-to-all | bytes 196608 | tf_op jit(solution)/shard_map/all_to_all | solution.py:339
  28.9 13.8 %all_to_all.16.received = f32[8,3,4,128]{3,2,1,0:T(4,128)S(1)} all-to-all(f32[8,3,4,128]{3,2,1,0:T(4,128)S(1)} %merge_stats.1), channel_id=1, replica_groups=mesh['x2'=2,'x1'=2,'x0'=2,'z2'=2,'z1'=2,'z0'=2,'y2'=2,'y1'=2,'y0'=2,'cor..., dimensions={0} | all-to-all | bytes 98304 | tf_op jit(solution)/shard_map/all_to_all | solution.py:347
  42.6 0.1 token_values.1
  42.7 12.8 %all_to_all.17 = f32[8,1,128]{2,1,0:T(1,128)S(1)} all-to-all(f32[8,1,128]{2,1,0:T(1,128)S(1)} %bitcast.12), channel_id=1, replica_groups=mesh['x2'=2,'x1'=2,'x0'=2,'z2'=2,'z1'=2,'z0'=2,'y2'=2,'y1'=2,'y0'=2,'cor..., dimensions={0} | all-to-all | bytes 8192 | tf_op jit(solution)/shard_map/all_to_all | solution.py:356
  55.5 0.8 %group_values.1 = (f32[1,8]{1,0:T(1,128)}, f32[4,128]{1,0:T(4,128)}, f32[4,128]{1,0:T(4,128)}, f32[4,128]{1,0:T(4,128)}, f32[1,1]{1,0:T(1,128)}) custom-call(f32[8,128]{1,0:T(8,128)S(1)} %bitcast.11, f32[3,8,128]{2,1,0:T(8,128)S(1)} %get-tuple-element.16.token_info, f32[8,128]{1,0:T(8,128)S(1)} %get-tuple-element.19.token_values), custom_call_target="tpu_custom_call" | custom-call | tf_op jit(solution)/shard_map/group_values/pallas_call | solution.py:357
  (1 shorter events, 0.0 us)

commit v8 on v7

--- a/solution.py
+++ b/solution.py
@@ -16,12 +16,26 @@
 Z_AXES = ("z2", "z1", "z0")
 Y_AXES = ("y2", "y1", "y0")
 MP = Z_AXES + Y_AXES + ("core",)
-FIRST = ("z0", "z1", "z2", "core")
-SECOND = ("y0", "y1", "y2")
-THIRD = ("x0", "x1", "x2")
+FIRST = Z_AXES + ("core",)
+SECOND = Y_AXES
 
 spread_floor = 0.25
 reward_unit = 1024.0
+
+
+def dp_groups():
+    groups = []
+    for z in range(8):
+        for y in range(8):
+            swapped = 1 if y == z == 0 else 0
+            for core in range(2):
+                groups.append(
+                    [
+                        ((x * 8 + z) * 8 + y) * 2 + (1 - core if x == swapped else core)
+                        for x in range(8)
+                    ]
+                )
+    return groups
 
 
 def lane_of(shape):
@@ -345,7 +359,7 @@
         out_shape=kept(2 ** len(SECOND), 3, chunks, LANES),
     )(near(received))
     received = lax.all_to_all(sent, SECOND, 0, 0, tiled=True)
-    shard_count = 2 ** len(THIRD)
+    shard_count = 2 ** len(X_AXES)
     sent, token_values = pl.pallas_call(
         token_kernel,
         name="token_values",
@@ -353,7 +367,14 @@
         out_specs=[vmem] * 2,
         out_shape=[kept(SUBLANES, LANES), kept(2 * chunks, LANES)],
     )(near(received), near(token_info), near(own_info))
-    received = lax.all_to_all(sent.reshape(shard_count, 1, LANES), THIRD, 0, 0, tiled=True)
+    received = lax.all_to_all(
+        sent.reshape(shard_count, 1, LANES),
+        X_AXES + MP,
+        0,
+        0,
+        axis_index_groups=dp_groups(),
+        tiled=True,
+    )
     advantage, token_weight, token_logprob, token_entropy, objective = pl.pallas_call(
         final_kernel,
         name="group_values",

time: 57.1 us -> 57.4 us (level)
  no operation moved by 1% of the time
where the time goes in v8:
time: 57.4 us; the launch traced here: 56.7 us
  blocking collectives  53.3 us (93%)
  Pallas kernels  2.76 us (5%)
  between operations  0.64 us (1%)
    all_to_all x1, blocking collectives, shards(): received = lax.all_to_all(sent, FIRST, 0, 0, tiled=True)  26.4 us
    all_to_all x1, blocking collectives, shards(): received = lax.all_to_all(sent, SECOND, 0, 0, tiled=True)  14.1 us
    all_to_all x1, blocking collectives, shards(): lax.all_to_all(sent.reshape(shard_count, 1, LANES), X_AXES + MP, 0, 0, ax...  12.8 us
    pallas_call x1, Pallas kernels, shards(): pl.pallas_call(local_kernel, name='local_stats', in_specs=[any_spec] * 6,...  1.77 us

profile of v8, /device:TPU:1, one launch (start us, length us, event | category | flops | bytes accessed | tf_op | source)
XLA Modules:
  0.0 56.7 jit_solution(12311967300584529609)
XLA Ops:
  0.6 1.8 %local_stats.1 = (f32[16,3,4,128]{3,2,1,0:T(4,128)S(1)}, f32[3,8,128]{2,1,0:T(8,128)S(1)}, f32[2,8,128]{2,1,0:T(8,128)S(1)}) custom-call(s32[8]{0:T(128)} %rewards.1, s32[8]{0:T(128)} %group_ids.1, s32[8]{0:T(128)} %lengths.1, s32[4,128]{1,0:T(4,128)} %bitcast.13, s32[4,128]{1,0:T(4,128)} %bitcast.14, bf16[512,512]{1,0:T(8,128)(2,1)} %logits.1), custom_call_target="tpu_custom_call" | custom-call | tf_op jit(solution)/shard_map/local_stats/pallas_call | solution.py:324
  2.4 26.4 %all_to_all.15.received = f32[16,3,4,128]{3,2,1,0:T(4,128)S(1)} all-to-all(f32[16,3,4,128]{3,2,1,0:T(4,128)S(1)} %get-tuple-element.15), channel_id=1, replica_groups=mesh['x2'=2,'x1'=2,'x0'=2,'z2'=2,'z1'=2,'z0'=2,'y2'=2,'y1'=2,'y0'=2,'cor..., dimensions={0} | all-to-all | bytes 196608 | tf_op jit(solution)/shard_map/all_to_all | solution.py:353
  28.9 14.1 %all_to_all.16.received = f32[8,3,4,128]{3,2,1,0:T(4,128)S(1)} all-to-all(f32[8,3,4,128]{3,2,1,0:T(4,128)S(1)} %merge_stats.1), channel_id=1, replica_groups=mesh['x2'=2,'x1'=2,'x0'=2,'z2'=2,'z1'=2,'z0'=2,'y2'=2,'y1'=2,'y0'=2,'cor..., dimensions={0} | all-to-all | bytes 98304 | tf_op jit(solution)/shard_map/all_to_all | solution.py:361
  43.0 0.1 token_values.1
  43.1 12.8 %all_to_all.17 = f32[8,1,128]{2,1,0:T(1,128)S(1)} all-to-all(f32[8,1,128]{2,1,0:T(1,128)S(1)} %bitcast.12), channel_id=1, replica_groups={{0,129,256,384,512,640,768,896},{1,128,257,385,513,641,769,897},{3,130,..., dimensions={0} | all-to-all | bytes 8192 | tf_op jit(solution)/shard_map/all_to_all | solution.py:370
  55.9 0.8 %group_values.1 = (f32[1,8]{1,0:T(1,128)}, f32[4,128]{1,0:T(4,128)}, f32[4,128]{1,0:T(4,128)}, f32[4,128]{1,0:T(4,128)}, f32[1,1]{1,0:T(1,128)}) custom-call(f32[8,128]{1,0:T(8,128)S(1)} %bitcast.11, f32[3,8,128]{2,1,0:T(8,128)S(1)} %get-tuple-element.16.token_info, f32[8,128]{1,0:T(8,128)S(1)} %get-tuple-element.19.token_values), custom_call_target="tpu_custom_call" | custom-call | tf_op jit(solution)/shard_map/group_values/pallas_call | solution.py:378
  (1 shorter events, 0.0 us)

commit v9 on v8

--- a/solution.py
+++ b/solution.py
@@ -16,24 +16,33 @@
 Z_AXES = ("z2", "z1", "z0")
 Y_AXES = ("y2", "y1", "y0")
 MP = Z_AXES + Y_AXES + ("core",)
-FIRST = Z_AXES + ("core",)
-SECOND = Y_AXES
+FIRST = ("core",) + Z_AXES
 
 spread_floor = 0.25
 reward_unit = 1024.0
 
 
-def dp_groups():
+def position(x, z, y, core):
+    return ((x * 8 + z) * 8 + y) * 2 + core
+
+
+def y_groups():
+    return [
+        [position(x, z, y, core if y < 4 else 1 - core) for y in range(8)]
+        for x in range(8)
+        for z in range(8)
+        for core in range(2)
+    ]
+
+
+def x_groups():
     groups = []
     for z in range(8):
         for y in range(8):
-            swapped = 1 if y == z == 0 else 0
+            swapped = (1,) if y == z == 0 else (4, 5, 6, 7)
             for core in range(2):
                 groups.append(
-                    [
-                        ((x * 8 + z) * 8 + y) * 2 + (1 - core if x == swapped else core)
-                        for x in range(8)
-                    ]
+                    [position(x, z, y, 1 - core if x in swapped else core) for x in range(8)]
                 )
     return groups
 
@@ -356,9 +365,11 @@
         name="merge_stats",
         in_specs=[vmem],
         out_specs=vmem,
-        out_shape=kept(2 ** len(SECOND), 3, chunks, LANES),
+        out_shape=kept(2 ** len(Y_AXES), 3, chunks, LANES),
     )(near(received))
-    received = lax.all_to_all(sent, SECOND, 0, 0, tiled=True)
+    received = lax.all_to_all(
+        sent, X_AXES + MP, 0, 0, axis_index_groups=y_groups(), tiled=True
+    )
     shard_count = 2 ** len(X_AXES)
     sent, token_values = pl.pallas_call(
         token_kernel,
@@ -372,7 +383,7 @@
         X_AXES + MP,
         0,
         0,
-        axis_index_groups=dp_groups(),
+        axis_index_groups=x_groups(),
         tiled=True,
     )
     advantage, token_weight, token_logprob, token_entropy, objective = pl.pallas_call(

time: 57.4 us -> 57.4 us (level)
    all_to_all x1, blocking collectives: 14.1 us -> 15.6 us  [shards(): lax.all_to_all(sent, X_AXES + MP, 0, 0, axis_index_groups=y_groups(), til...]
    all_to_all x1, blocking collectives: 26.4 us -> 25.3 us  [shards(): received = lax.all_to_all(sent, FIRST, 0, 0, tiled=True)]
where the time goes in v9:
time: 57.4 us; the launch traced here: 57.2 us
  blocking collectives  53.8 us (94%)
  Pallas kernels  2.76 us (5%)
  between operations  0.64 us (1%)
    all_to_all x1, blocking collectives, shards(): received = lax.all_to_all(sent, FIRST, 0, 0, tiled=True)  25.3 us
    all_to_all x1, blocking collectives, shards(): lax.all_to_all(sent, X_AXES + MP, 0, 0, axis_index_groups=y_groups(), til...  15.6 us
    all_to_all x1, blocking collectives, shards(): lax.all_to_all(sent.reshape(shard_count, 1, LANES), X_AXES + MP, 0, 0, ax...  12.9 us
    pallas_call x1, Pallas kernels, shards(): pl.pallas_call(local_kernel, name='local_stats', in_specs=[any_spec] * 6,...  1.77 us

profile of v9, /device:TPU:1, one launch (start us, length us, event | category | flops | bytes accessed | tf_op | source)
XLA Modules:
  0.0 57.2 jit_solution(17154926409248567001)
XLA Ops:
  0.6 1.8 %local_stats.1 = (f32[16,3,4,128]{3,2,1,0:T(4,128)S(1)}, f32[3,8,128]{2,1,0:T(8,128)S(1)}, f32[2,8,128]{2,1,0:T(8,128)S(1)}) custom-call(s32[8]{0:T(128)} %rewards.1, s32[8]{0:T(128)} %group_ids.1, s32[8]{0:T(128)} %lengths.1, s32[4,128]{1,0:T(4,128)} %bitcast.13, s32[4,128]{1,0:T(4,128)} %bitcast.14, bf16[512,512]{1,0:T(8,128)(2,1)} %logits.1), custom_call_target="tpu_custom_call" | custom-call | tf_op jit(solution)/shard_map/local_stats/pallas_call | solution.py:333
  2.4 25.3 %all_to_all.15.received = f32[16,3,4,128]{3,2,1,0:T(4,128)S(1)} all-to-all(f32[16,3,4,128]{3,2,1,0:T(4,128)S(1)} %get-tuple-element.15), channel_id=1, replica_groups=mesh['x2'=2,'x1'=2,'x0'=2,'z2'=2,'z1'=2,'z0'=2,'y2'=2,'y1'=2,'y0'=2,'cor..., dimensions={0} | all-to-all | bytes 196608 | tf_op jit(solution)/shard_map/all_to_all | solution.py:362
  27.8 15.6 %all_to_all.16.received = f32[8,3,4,128]{3,2,1,0:T(4,128)S(1)} all-to-all(f32[8,3,4,128]{3,2,1,0:T(4,128)S(1)} %merge_stats.1), channel_id=1, replica_groups={{0,2,4,6,9,11,13,15},{1,3,5,7,8,10,12,14},{16,18,20,22,25,27,29,31},{17..., dimensions={0} | all-to-all | bytes 98304 | tf_op jit(solution)/shard_map/all_to_all | solution.py:370
  43.4 0.1 token_values.1
  43.5 12.9 %all_to_all.17 = f32[8,1,128]{2,1,0:T(1,128)S(1)} all-to-all(f32[8,1,128]{2,1,0:T(1,128)S(1)} %bitcast.12), channel_id=1, replica_groups={{0,129,256,384,512,640,768,896},{1,128,257,385,513,641,769,897},{2,130,..., dimensions={0} | all-to-all | bytes 8192 | tf_op jit(solution)/shard_map/all_to_all | solution.py:381
  56.4 0.8 %group_values.1 = (f32[1,8]{1,0:T(1,128)}, f32[4,128]{1,0:T(4,128)}, f32[4,128]{1,0:T(4,128)}, f32[4,128]{1,0:T(4,128)}, f32[1,1]{1,0:T(1,128)}) custom-call(f32[8,128]{1,0:T(8,128)S(1)} %bitcast.11, f32[3,8,128]{2,1,0:T(8,128)S(1)} %get-tuple-element.16.token_info, f32[8,128]{1,0:T(8,128)S(1)} %get-tuple-element.19.token_values), custom_call_target="tpu_custom_call" | custom-call | tf_op jit(solution)/shard_map/group_values/pallas_call | solution.py:389
  (1 shorter events, 0.0 us)

commit v10 on v9

--- a/solution.py
+++ b/solution.py
@@ -39,7 +39,7 @@
     groups = []
     for z in range(8):
         for y in range(8):
-            swapped = (1,) if y == z == 0 else (4, 5, 6, 7)
+            swapped = () if y == z == 0 else (4, 5, 6, 7)
             for core in range(2):
                 groups.append(
                     [position(x, z, y, 1 - core if x in swapped else core) for x in range(8)]

time: 57.4 us -> 57.4 us (level)
  no operation moved by 1% of the time
where the time goes in v10:
time: 57.4 us; the launch traced here: 57.2 us
  blocking collectives  53.8 us (94%)
  Pallas kernels  2.76 us (5%)
  between operations  0.64 us (1%)
    all_to_all x1, blocking collectives, shards(): received = lax.all_to_all(sent, FIRST, 0, 0, tiled=True)  25.3 us
    all_to_all x1, blocking collectives, shards(): lax.all_to_all(sent, X_AXES + MP, 0, 0, axis_index_groups=y_groups(), til...  15.6 us
    all_to_all x1, blocking collectives, shards(): lax.all_to_all(sent.reshape(shard_count, 1, LANES), X_AXES + MP, 0, 0, ax...  12.8 us
    pallas_call x1, Pallas kernels, shards(): pl.pallas_call(local_kernel, name='local_stats', in_specs=[any_spec] * 6,...  1.77 us

profile of v10, /device:TPU:1, one launch (start us, length us, event | category | flops | bytes accessed | tf_op | source)
XLA Modules:
  0.0 57.2 jit_solution(7400700220481006635)
XLA Ops:
  0.6 1.8 %local_stats.1 = (f32[16,3,4,128]{3,2,1,0:T(4,128)S(1)}, f32[3,8,128]{2,1,0:T(8,128)S(1)}, f32[2,8,128]{2,1,0:T(8,128)S(1)}) custom-call(s32[8]{0:T(128)} %rewards.1, s32[8]{0:T(128)} %group_ids.1, s32[8]{0:T(128)} %lengths.1, s32[4,128]{1,0:T(4,128)} %bitcast.13, s32[4,128]{1,0:T(4,128)} %bitcast.14, bf16[512,512]{1,0:T(8,128)(2,1)} %logits.1), custom_call_target="tpu_custom_call" | custom-call | tf_op jit(solution)/shard_map/local_stats/pallas_call | solution.py:333
  2.4 25.3 %all_to_all.15.received = f32[16,3,4,128]{3,2,1,0:T(4,128)S(1)} all-to-all(f32[16,3,4,128]{3,2,1,0:T(4,128)S(1)} %get-tuple-element.15), channel_id=1, replica_groups=mesh['x2'=2,'x1'=2,'x0'=2,'z2'=2,'z1'=2,'z0'=2,'y2'=2,'y1'=2,'y0'=2,'cor..., dimensions={0} | all-to-all | bytes 196608 | tf_op jit(solution)/shard_map/all_to_all | solution.py:362
  27.8 15.6 %all_to_all.16.received = f32[8,3,4,128]{3,2,1,0:T(4,128)S(1)} all-to-all(f32[8,3,4,128]{3,2,1,0:T(4,128)S(1)} %merge_stats.1), channel_id=1, replica_groups={{0,2,4,6,9,11,13,15},{1,3,5,7,8,10,12,14},{16,18,20,22,25,27,29,31},{17..., dimensions={0} | all-to-all | bytes 98304 | tf_op jit(solution)/shard_map/all_to_all | solution.py:370
  43.4 0.1 token_values.1
  43.5 12.8 %all_to_all.17 = f32[8,1,128]{2,1,0:T(1,128)S(1)} all-to-all(f32[8,1,128]{2,1,0:T(1,128)S(1)} %bitcast.12), channel_id=1, replica_groups={{0,128,256,384,512,640,768,896},{1,129,257,385,513,641,769,897},{2,130,..., dimensions={0} | all-to-all | bytes 8192 | tf_op jit(solution)/shard_map/all_to_all | solution.py:381
  56.3 0.8 %group_values.1 = (f32[1,8]{1,0:T(1,128)}, f32[4,128]{1,0:T(4,128)}, f32[4,128]{1,0:T(4,128)}, f32[4,128]{1,0:T(4,128)}, f32[1,1]{1,0:T(1,128)}) custom-call(f32[8,128]{1,0:T(8,128)S(1)} %bitcast.11, f32[3,8,128]{2,1,0:T(8,128)S(1)} %get-tuple-element.16.token_info, f32[8,128]{1,0:T(8,128)S(1)} %get-tuple-element.19.token_values), custom_call_target="tpu_custom_call" | custom-call | tf_op jit(solution)/shard_map/group_values/pallas_call | solution.py:389
  (1 shorter events, 0.0 us)

commit v11 on v10

--- a/solution.py
+++ b/solution.py
@@ -28,7 +28,7 @@
 
 def y_groups():
     return [
-        [position(x, z, y, core if y < 4 else 1 - core) for y in range(8)]
+        [position(x, z, y, core if y < 4 or z == 0 else 1 - core) for y in range(8)]
         for x in range(8)
         for z in range(8)
         for core in range(2)
@@ -36,15 +36,18 @@
 
 
 def x_groups():
-    groups = []
+    groups = {}
     for z in range(8):
         for y in range(8):
-            swapped = () if y == z == 0 else (4, 5, 6, 7)
+            swapped = (4, 5, 6, 7) if z else (4,) if y else ()
             for core in range(2):
-                groups.append(
-                    [position(x, z, y, 1 - core if x in swapped else core) for x in range(8)]
-                )
-    return groups
+                groups[z, y, core] = [
+                    position(x, z, y, 1 - core if x in swapped else core) for x in range(8)
+                ]
+    here, there = groups[0, 0, 0], groups[1, 0, 0]
+    for x in (3, 4, 5):
+        here[x], there[x] = there[x], here[x]
+    return list(groups.values())
 
 
 def lane_of(shape):

time: 57.4 us -> 57.5 us (level)
  the two profiles are of different devices: /device:TPU:1 before, /device:TPU:2 now
where the time goes in v11:
time: 57.5 us; the launch traced here: 57.3 us
  blocking collectives  53.9 us (94%)
  Pallas kernels  2.76 us (5%)
  between operations  0.64 us (1%)
    all_to_all x1, blocking collectives, shards(): received = lax.all_to_all(sent, FIRST, 0, 0, tiled=True)  24.9 us
    all_to_all x1, blocking collectives, shards(): lax.all_to_all(sent, X_AXES + MP, 0, 0, axis_index_groups=y_groups(), til...  15.6 us
    all_to_all x1, blocking collectives, shards(): lax.all_to_all(sent.reshape(shard_count, 1, LANES), X_AXES + MP, 0, 0, ax...  13.4 us
    pallas_call x1, Pallas kernels, shards(): pl.pallas_call(local_kernel, name='local_stats', in_specs=[any_spec] * 6,...  1.77 us

profile of v11, /device:TPU:2, one launch (start us, length us, event | category | flops | bytes accessed | tf_op | source)
XLA Modules:
  0.0 57.3 jit_solution(16918337914301424550)
XLA Ops:
  0.6 1.8 %local_stats.1 = (f32[16,3,4,128]{3,2,1,0:T(4,128)S(1)}, f32[3,8,128]{2,1,0:T(8,128)S(1)}, f32[2,8,128]{2,1,0:T(8,128)S(1)}) custom-call(s32[8]{0:T(128)} %rewards.1, s32[8]{0:T(128)} %group_ids.1, s32[8]{0:T(128)} %lengths.1, s32[4,128]{1,0:T(4,128)} %bitcast.13, s32[4,128]{1,0:T(4,128)} %bitcast.14, bf16[512,512]{1,0:T(8,128)(2,1)} %logits.1), custom_call_target="tpu_custom_call" | custom-call | tf_op jit(solution)/shard_map/local_stats/pallas_call | solution.py:336
  2.4 24.9 %all_to_all.15.received = f32[16,3,4,128]{3,2,1,0:T(4,128)S(1)} all-to-all(f32[16,3,4,128]{3,2,1,0:T(4,128)S(1)} %get-tuple-element.15), channel_id=1, replica_groups=mesh['x2'=2,'x1'=2,'x0'=2,'z2'=2,'z1'=2,'z0'=2,'y2'=2,'y1'=2,'y0'=2,'cor..., dimensions={0} | all-to-all | bytes 196608 | tf_op jit(solution)/shard_map/all_to_all | solution.py:365
  27.4 15.6 %all_to_all.16.received = f32[8,3,4,128]{3,2,1,0:T(4,128)S(1)} all-to-all(f32[8,3,4,128]{3,2,1,0:T(4,128)S(1)} %merge_stats.1), channel_id=1, replica_groups={{0,2,4,6,8,10,12,14},{1,3,5,7,9,11,13,15},{16,18,20,22,25,27,29,31},{17..., dimensions={0} | all-to-all | bytes 98304 | tf_op jit(solution)/shard_map/all_to_all | solution.py:373
  42.9 0.1 token_values.1
  43.0 13.4 %all_to_all.17 = f32[8,1,128]{2,1,0:T(1,128)S(1)} all-to-all(f32[8,1,128]{2,1,0:T(1,128)S(1)} %bitcast.12), channel_id=1, replica_groups={{0,128,256,400,529,657,768,896},{1,129,257,385,513,641,769,897},{2,130,..., dimensions={0} | all-to-all | bytes 8192 | tf_op jit(solution)/shard_map/all_to_all | solution.py:384
  56.4 0.8 %group_values.1 = (f32[1,8]{1,0:T(1,128)}, f32[4,128]{1,0:T(4,128)}, f32[4,128]{1,0:T(4,128)}, f32[4,128]{1,0:T(4,128)}, f32[1,1]{1,0:T(1,128)}) custom-call(f32[8,128]{1,0:T(8,128)S(1)} %bitcast.11, f32[3,8,128]{2,1,0:T(8,128)S(1)} %get-tuple-element.16.token_info, f32[8,128]{1,0:T(8,128)S(1)} %get-tuple-element.19.token_values), custom_call_target="tpu_custom_call" | custom-call | tf_op jit(solution)/shard_map/group_values/pallas_call | solution.py:392
  (1 shorter events, 0.0 us)

commit v12 on v10

--- a/solution.py
+++ b/solution.py
@@ -28,7 +28,7 @@
 
 def y_groups():
     return [
-        [position(x, z, y, core if y < 4 else 1 - core) for y in range(8)]
+        [position(x, z, y, 1 - core if y in ((4, 5, 6, 7) if z else (4,)) else core) for y in range(8)]
         for x in range(8)
         for z in range(8)
         for core in range(2)

time: 57.4 us -> 57.5 us (level)
  no operation moved by 1% of the time
where the time goes in v12:
time: 57.5 us; the launch traced here: 57.2 us
  blocking collectives  53.8 us (94%)
  Pallas kernels  2.76 us (5%)
  between operations  0.64 us (1%)
    all_to_all x1, blocking collectives, shards(): received = lax.all_to_all(sent, FIRST, 0, 0, tiled=True)  25.3 us
    all_to_all x1, blocking collectives, shards(): lax.all_to_all(sent, X_AXES + MP, 0, 0, axis_index_groups=y_groups(), til...  15.6 us
    all_to_all x1, blocking collectives, shards(): lax.all_to_all(sent.reshape(shard_count, 1, LANES), X_AXES + MP, 0, 0, ax...  12.8 us
    pallas_call x1, Pallas kernels, shards(): pl.pallas_call(local_kernel, name='local_stats', in_specs=[any_spec] * 6,...  1.77 us

profile of v12, /device:TPU:1, one launch (start us, length us, event | category | flops | bytes accessed | tf_op | source)
XLA Modules:
  0.0 57.2 jit_solution(12386456520849115370)
XLA Ops:
  0.6 1.8 %local_stats.1 = (f32[16,3,4,128]{3,2,1,0:T(4,128)S(1)}, f32[3,8,128]{2,1,0:T(8,128)S(1)}, f32[2,8,128]{2,1,0:T(8,128)S(1)}) custom-call(s32[8]{0:T(128)} %rewards.1, s32[8]{0:T(128)} %group_ids.1, s32[8]{0:T(128)} %lengths.1, s32[4,128]{1,0:T(4,128)} %bitcast.13, s32[4,128]{1,0:T(4,128)} %bitcast.14, bf16[512,512]{1,0:T(8,128)(2,1)} %logits.1), custom_call_target="tpu_custom_call" | custom-call | tf_op jit(solution)/shard_map/local_stats/pallas_call | solution.py:333
  2.4 25.3 %all_to_all.15.received = f32[16,3,4,128]{3,2,1,0:T(4,128)S(1)} all-to-all(f32[16,3,4,128]{3,2,1,0:T(4,128)S(1)} %get-tuple-element.15), channel_id=1, replica_groups=mesh['x2'=2,'x1'=2,'x0'=2,'z2'=2,'z1'=2,'z0'=2,'y2'=2,'y1'=2,'y0'=2,'cor..., dimensions={0} | all-to-all | bytes 196608 | tf_op jit(solution)/shard_map/all_to_all | solution.py:362
  27.8 15.6 %all_to_all.16.received = f32[8,3,4,128]{3,2,1,0:T(4,128)S(1)} all-to-all(f32[8,3,4,128]{3,2,1,0:T(4,128)S(1)} %merge_stats.1), channel_id=1, replica_groups={{0,2,4,6,9,10,12,14},{1,3,5,7,8,11,13,15},{16,18,20,22,25,27,29,31},{17..., dimensions={0} | all-to-all | bytes 98304 | tf_op jit(solution)/shard_map/all_to_all | solution.py:370
  43.4 0.1 token_values.1
  43.6 12.8 %all_to_all.17 = f32[8,1,128]{2,1,0:T(1,128)S(1)} all-to-all(f32[8,1,128]{2,1,0:T(1,128)S(1)} %bitcast.12), channel_id=1, replica_groups={{0,128,256,384,512,640,768,896},{1,129,257,385,513,641,769,897},{2,130,..., dimensions={0} | all-to-all | bytes 8192 | tf_op jit(solution)/shard_map/all_to_all | solution.py:381
  56.4 0.8 %group_values.1 = (f32[1,8]{1,0:T(1,128)}, f32[4,128]{1,0:T(4,128)}, f32[4,128]{1,0:T(4,128)}, f32[4,128]{1,0:T(4,128)}, f32[1,1]{1,0:T(1,128)}) custom-call(f32[8,128]{1,0:T(8,128)S(1)} %bitcast.11, f32[3,8,128]{2,1,0:T(8,128)S(1)} %get-tuple-element.16.token_info, f32[8,128]{1,0:T(8,128)S(1)} %get-tuple-element.19.token_values), custom_call_target="tpu_custom_call" | custom-call | tf_op jit(solution)/shard_map/group_values/pallas_call | solution.py:389
  (1 shorter events, 0.0 us)

commit v13 on v7

--- a/solution.py
+++ b/solution.py
@@ -16,9 +16,9 @@
 Z_AXES = ("z2", "z1", "z0")
 Y_AXES = ("y2", "y1", "y0")
 MP = Z_AXES + Y_AXES + ("core",)
-FIRST = ("z0", "z1", "z2", "core")
-SECOND = ("y0", "y1", "y2")
-THIRD = ("x0", "x1", "x2")
+FIRST = Z_AXES + ("core",)
+SECOND = Y_AXES
+THIRD = X_AXES
 
 spread_floor = 0.25
 reward_unit = 1024.0

time: 57.1 us -> 57.4 us (level)
  no operation moved by 1% of the time
where the time goes in v13:
time: 57.4 us; the launch traced here: 56.7 us
  blocking collectives  53.3 us (93%)
  Pallas kernels  2.76 us (5%)
  between operations  0.64 us (1%)
    all_to_all x1, blocking collectives, shards(): received = lax.all_to_all(sent, FIRST, 0, 0, tiled=True)  26.4 us
    all_to_all x1, blocking collectives, shards(): received = lax.all_to_all(sent, SECOND, 0, 0, tiled=True)  14.1 us
    all_to_all x1, blocking collectives, shards(): lax.all_to_all(sent.reshape(shard_count, 1, LANES), THIRD, 0, 0, tiled=True)  12.8 us
    pallas_call x1, Pallas kernels, shards(): pl.pallas_call(local_kernel, name='local_stats', in_specs=[any_spec] * 6,...  1.77 us

profile of v13, /device:TPU:1, one launch (start us, length us, event | category | flops | bytes accessed | tf_op | source)
XLA Modules:
  0.0 56.7 jit_solution(11626718645085133425)
XLA Ops:
  0.6 1.8 %local_stats.1 = (f32[16,3,4,128]{3,2,1,0:T(4,128)S(1)}, f32[3,8,128]{2,1,0:T(8,128)S(1)}, f32[2,8,128]{2,1,0:T(8,128)S(1)}) custom-call(s32[8]{0:T(128)} %rewards.1, s32[8]{0:T(128)} %group_ids.1, s32[8]{0:T(128)} %lengths.1, s32[4,128]{1,0:T(4,128)} %bitcast.13, s32[4,128]{1,0:T(4,128)} %bitcast.14, bf16[512,512]{1,0:T(8,128)(2,1)} %logits.1), custom_call_target="tpu_custom_call" | custom-call | tf_op jit(solution)/shard_map/local_stats/pallas_call | solution.py:310
  2.4 26.4 %all_to_all.15.received = f32[16,3,4,128]{3,2,1,0:T(4,128)S(1)} all-to-all(f32[16,3,4,128]{3,2,1,0:T(4,128)S(1)} %get-tuple-element.15), channel_id=1, replica_groups=mesh['x2'=2,'x1'=2,'x0'=2,'z2'=2,'z1'=2,'z0'=2,'y2'=2,'y1'=2,'y0'=2,'cor..., dimensions={0} | all-to-all | bytes 196608 | tf_op jit(solution)/shard_map/all_to_all | solution.py:339
  28.9 14.1 %all_to_all.16.received = f32[8,3,4,128]{3,2,1,0:T(4,128)S(1)} all-to-all(f32[8,3,4,128]{3,2,1,0:T(4,128)S(1)} %merge_stats.1), channel_id=1, replica_groups=mesh['x2'=2,'x1'=2,'x0'=2,'z2'=2,'z1'=2,'z0'=2,'y2'=2,'y1'=2,'y0'=2,'cor..., dimensions={0} | all-to-all | bytes 98304 | tf_op jit(solution)/shard_map/all_to_all | solution.py:347
  43.0 0.1 token_values.1
  43.1 12.8 %all_to_all.17 = f32[8,1,128]{2,1,0:T(1,128)S(1)} all-to-all(f32[8,1,128]{2,1,0:T(1,128)S(1)} %bitcast.12), channel_id=1, replica_groups=mesh['x2'=2,'x1'=2,'x0'=2,'z2'=2,'z1'=2,'z0'=2,'y2'=2,'y1'=2,'y0'=2,'cor..., dimensions={0} | all-to-all | bytes 8192 | tf_op jit(solution)/shard_map/all_to_all | solution.py:356
  55.9 0.8 %group_values.1 = (f32[1,8]{1,0:T(1,128)}, f32[4,128]{1,0:T(4,128)}, f32[4,128]{1,0:T(4,128)}, f32[4,128]{1,0:T(4,128)}, f32[1,1]{1,0:T(1,128)}) custom-call(f32[8,128]{1,0:T(8,128)S(1)} %bitcast.11, f32[3,8,128]{2,1,0:T(8,128)S(1)} %get-tuple-element.16.token_info, f32[8,128]{1,0:T(8,128)S(1)} %get-tuple-element.19.token_values), custom_call_target="tpu_custom_call" | custom-call | tf_op jit(solution)/shard_map/group_values/pallas_call | solution.py:357
  (1 shorter events, 0.0 us)

commit v14 on v13

--- a/solution.py
+++ b/solution.py
@@ -281,15 +281,15 @@
         mean = jnp.where(chosen, group_mean[g : g + 1], mean)
         spread = jnp.where(chosen, one_spread, spread)
         tokens = jnp.where(chosen, one_tokens, tokens)
-    total_rows = GROUPS * GROUP * WIN
-    objective_row[...] = -terms / total_rows
-    copies[4].start()
     info_advantage = (info_reward - mean) / spread
     weight = token_info[0] * (info_advantage * (GROUP * WIN / tokens))
     advantage_row[...] = info_advantage[chunks : chunks + 1, :SUBLANES]
     copies[3].start()
     weight_rows[...] = weight[:chunks]
     copies[2].start()
+    total_rows = GROUPS * GROUP * WIN
+    objective_row[...] = -terms / total_rows
+    copies[4].start()
     for copy in copies:
         copy.wait()
 

time: 57.4 us -> 57.4 us (level)
  no operation moved by 1% of the time
where the time goes in v14:
time: 57.4 us; the launch traced here: 56.7 us
  blocking collectives  53.3 us (93%)
  Pallas kernels  2.76 us (5%)
  between operations  0.64 us (1%)
    all_to_all x1, blocking collectives, shards(): received = lax.all_to_all(sent, FIRST, 0, 0, tiled=True)  26.4 us
    all_to_all x1, blocking collectives, shards(): received = lax.all_to_all(sent, SECOND, 0, 0, tiled=True)  14.1 us
    all_to_all x1, blocking collectives, shards(): lax.all_to_all(sent.reshape(shard_count, 1, LANES), THIRD, 0, 0, tiled=True)  12.8 us
    pallas_call x1, Pallas kernels, shards(): pl.pallas_call(local_kernel, name='local_stats', in_specs=[any_spec] * 6,...  1.77 us

profile of v14, /device:TPU:1, one launch (start us, length us, event | category | flops | bytes accessed | tf_op | source)
XLA Modules:
  0.0 56.7 jit_solution(18368347616312443090)
XLA Ops:
  0.6 1.8 %local_stats.1 = (f32[16,3,4,128]{3,2,1,0:T(4,128)S(1)}, f32[3,8,128]{2,1,0:T(8,128)S(1)}, f32[2,8,128]{2,1,0:T(8,128)S(1)}) custom-call(s32[8]{0:T(128)} %rewards.1, s32[8]{0:T(128)} %group_ids.1, s32[8]{0:T(128)} %lengths.1, s32[4,128]{1,0:T(4,128)} %bitcast.13, s32[4,128]{1,0:T(4,128)} %bitcast.14, bf16[512,512]{1,0:T(8,128)(2,1)} %logits.1), custom_call_target="tpu_custom_call" | custom-call | tf_op jit(solution)/shard_map/local_stats/pallas_call | solution.py:310
  2.4 26.4 %all_to_all.15.received = f32[16,3,4,128]{3,2,1,0:T(4,128)S(1)} all-to-all(f32[16,3,4,128]{3,2,1,0:T(4,128)S(1)} %get-tuple-element.15), channel_id=1, replica_groups=mesh['x2'=2,'x1'=2,'x0'=2,'z2'=2,'z1'=2,'z0'=2,'y2'=2,'y1'=2,'y0'=2,'cor..., dimensions={0} | all-to-all | bytes 196608 | tf_op jit(solution)/shard_map/all_to_all | solution.py:339
  28.9 14.1 %all_to_all.16.received = f32[8,3,4,128]{3,2,1,0:T(4,128)S(1)} all-to-all(f32[8,3,4,128]{3,2,1,0:T(4,128)S(1)} %merge_stats.1), channel_id=1, replica_groups=mesh['x2'=2,'x1'=2,'x0'=2,'z2'=2,'z1'=2,'z0'=2,'y2'=2,'y1'=2,'y0'=2,'cor..., dimensions={0} | all-to-all | bytes 98304 | tf_op jit(solution)/shard_map/all_to_all | solution.py:347
  43.0 0.1 token_values.1
  43.1 12.8 %all_to_all.17 = f32[8,1,128]{2,1,0:T(1,128)S(1)} all-to-all(f32[8,1,128]{2,1,0:T(1,128)S(1)} %bitcast.12), channel_id=1, replica_groups=mesh['x2'=2,'x1'=2,'x0'=2,'z2'=2,'z1'=2,'z0'=2,'y2'=2,'y1'=2,'y0'=2,'cor..., dimensions={0} | all-to-all | bytes 8192 | tf_op jit(solution)/shard_map/all_to_all | solution.py:356
  55.9 0.8 %group_values.1 = (f32[1,8]{1,0:T(1,128)}, f32[4,128]{1,0:T(4,128)}, f32[4,128]{1,0:T(4,128)}, f32[4,128]{1,0:T(4,128)}, f32[1,1]{1,0:T(1,128)}) custom-call(f32[8,128]{1,0:T(8,128)S(1)} %bitcast.11, f32[3,8,128]{2,1,0:T(8,128)S(1)} %get-tuple-element.16.token_info, f32[8,128]{1,0:T(8,128)S(1)} %get-tuple-element.19.token_values), custom_call_target="tpu_custom_call" | custom-call | tf_op jit(solution)/shard_map/group_values/pallas_call | solution.py:357
  (1 shorter events, 0.0 us)
